TPU v7x, 32 devices: a whole 2x2x4 slice. The times are simulated.
32 devices in a mesh: role: 4 (over z), grp: 2 (over y), rep: 4 (over x, core).
Axes of the slice: x: 2, y: 2, z: 4, core: 2. Of those that a mesh axis runs over, the one named last changes fastest.
Arguments:
- facets: bfloat16 [4, 2, 4096, 4096], P('role', None, ('grp', 'rep')), may hold values from -6 to 6
- taper: float32 [4, 4096], P('role'), may hold values from 0.3 to 1.5
- kernel: float32 [8], replicated, may hold values from 0.1 to 0.5
- observed: float32 [2, 8, 16, 512], P(None, ('role', 'grp'), 'rep'), may hold values from -6 to 6
- patch_pos: int32 [8, 16], P(('role', 'grp'), 'rep'), may hold values from 0 to 23, as said below
- counts: int32 [8, 16], P(('role', 'grp'), 'rep'), may hold values from 1 to 512, 5120 in all within a row
- vis_u: int32 [8, 16, 512], P(('role', 'grp'), 'rep'), may hold values from 0 to 24
- vis_v: int32 [8, 16, 512], P(('role', 'grp'), 'rep'), may hold values from 0 to 24
Outputs:
- residual_vis: float32 [2, 8, 16, 512], P(None, ('role', 'grp'), 'rep')
- returned: bfloat16 [2, 8, 128, 128], P(None, None, ('grp', 'rep'))
Inputs may be any that keep to these rules, and one draw needn't show every extreme that they name: Visibility slots v < counts are live, the rest are padding; the counts of one subgrid's patches sum to 5120 and one of them equals 512. `patch_pos`: split the patches of a subgrid into 4 aligned runs of 4; in each run the first patch covers a block in the first column of blocks and the second a block in the last column of blocks, the others any block.
All inputs are finite; a program needn't handle non-finite values. No bound on the sum of `counts` on one device may be relied on, other than what follows from the above.
Results may differ from a plain program's by a relative error of at most 0.014.
Values may be sent and summed in bfloat16 or wider, within the bound.
No kernel may reach another device: no remote copies, remote signals or barrier semaphores. Data moves between devices by JAX's collectives and lax.ppermute only.
A program may use at most 64 MiB of HBM per device.

v0:
```python
import math

import jax
import numpy as np
import jax.numpy as jnp
from jax import lax
from jax.experimental import pallas as pl
from jax.experimental.pallas import tpu as pltpu
from jax.sharding import PartitionSpec as P


F = 4096
C = 128
PATCH = 32
EDGE = 32
KW = 8


def extended(block, sides, width):
    for axis, dim in sides:
        count = lax.axis_size(axis)
        forward = [(i, i + 1) for i in range(count - 1)]
        backward = [(target, source) for source, target in forward]
        low = lax.ppermute(
            lax.slice_in_dim(block, block.shape[dim] - width, None, axis=dim), axis, forward
        )
        high = lax.ppermute(lax.slice_in_dim(block, 0, width, axis=dim), axis, backward)
        block = jnp.concatenate([low, block, high], axis=dim)
    return block


def shifted(value, axis, by):
    size = lax.axis_size(axis)
    pairs = [(i, i + by) for i in range(size) if 0 <= i + by < size]
    return lax.ppermute(value, axis, pairs)


def phases(frequency, length):
    columns = jnp.arange(length, dtype=jnp.int32)
    product = frequency[:, None] * columns[None, :] % length
    angles = product.astype(jnp.float32) * (2.0 * math.pi / length)
    return (jnp.cos(angles), jnp.sin(angles))


def windowed(frequency, window):
    length = window.shape[0]
    wave_cos, wave_sin = phases(frequency, length)
    scale_norm = 1.0 / math.sqrt(length)
    table_re = (window[None, :] * wave_cos * scale_norm).astype(jnp.bfloat16)
    table_im = (-(window[None, :] * wave_sin) * scale_norm).astype(jnp.bfloat16)
    return (table_re, table_im)


def contract(left, right):
    return lax.dot_general(
        left, right, (((1,), (1,)), ((), ())), preferred_element_type=jnp.float32
    )


def project(table_re, table_im, data_re, data_im):
    part_re = contract(table_re, data_re) - contract(table_im, data_im)
    part_im = contract(table_re, data_im) + contract(table_im, data_re)
    return (part_re, part_im)


def modulate(part_re, part_im, wave_cos, wave_sin):
    mod_re = (part_re * wave_cos + part_im * wave_sin).astype(jnp.bfloat16)
    mod_im = (part_im * wave_cos - part_re * wave_sin).astype(jnp.bfloat16)
    return (mod_re, mod_im)


def kernel_rows(offsets, kernel):
    cell_index = jnp.arange(PATCH, dtype=jnp.int32)
    distance = cell_index[None, :, None] - offsets[:, None, :]
    result = jnp.zeros(distance.shape, jnp.float32)
    for position in range(KW):
        result = result + kernel[position] * (distance == position).astype(jnp.float32)
    return result


def degrid(widened, patch_pos, counts, vis_u, vis_v, observed, kernel):
    high = lax.Precision.HIGHEST
    row_blocks = widened.shape[1] // PATCH
    col_blocks = widened.shape[2] // PATCH
    blocks = widened.reshape(2, row_blocks, PATCH, col_blocks, PATCH).transpose(0, 1, 3, 2, 4)
    blocks = blocks.reshape(2, row_blocks * col_blocks, PATCH, PATCH)
    selected = jnp.take(blocks, patch_pos, axis=1).astype(jnp.float32)
    rows_u = kernel_rows(vis_u, kernel)
    rows_v = kernel_rows(vis_v, kernel)
    partial_value = jnp.einsum("cpab,pav->cpbv", selected, rows_u, precision=high)
    predicted = jnp.einsum("cpbv,pbv->cpv", partial_value, rows_v, precision=high)
    live_mask = (jnp.arange(observed.shape[-1], dtype=jnp.int32)[None, :] < counts[:, None]).astype(
        jnp.float32
    )
    residual = (observed - predicted) * live_mask[None]
    weighted = residual[:, :, None, :] * rows_v[None]
    gridded = jnp.einsum("pav,cpbv->cpab", rows_u, weighted, precision=high)
    one_hot = (
        patch_pos[:, None] == jnp.arange(row_blocks * col_blocks, dtype=jnp.int32)[None, :]
    ).astype(jnp.float32)
    placed = jnp.einsum("pq,cpab->cqab", one_hot, gridded, precision=high)
    regrid = placed.reshape(2, row_blocks, col_blocks, PATCH, PATCH).transpose(0, 1, 3, 2, 4)
    return (residual, regrid.reshape(2, widened.shape[1], widened.shape[2]))


def local(facets, taper, kernel, observed, patch_pos, counts, vis_u, vis_v):
    grp_count = lax.axis_size("grp")
    rep_count = lax.axis_size("rep")
    role_count = lax.axis_size("role")
    sub_cols = role_count * grp_count
    row_share = C // (grp_count * rep_count)
    strip_data = facets[0]
    window = taper[0]
    row_freq = jnp.arange(C, dtype=jnp.int32)
    table_re, table_im = windowed(row_freq, window)
    part_re, part_im = project(table_re, table_im, strip_data[0], strip_data[1])
    partial_value = jnp.stack([part_re, part_im]).astype(jnp.bfloat16)
    row_block = lax.all_to_all(
        partial_value, ("grp", "rep"), split_axis=1, concat_axis=2, tiled=True
    )
    shift_freq = jnp.arange(sub_cols, dtype=jnp.int32) * (F // sub_cols)
    wave_cos, wave_sin = phases(shift_freq, F)
    mod_re, mod_im = modulate(
        row_block[0][None].astype(jnp.float32),
        row_block[1][None].astype(jnp.float32),
        (window[None, :] * wave_cos)[:, None, :],
        (window[None, :] * wave_sin)[:, None, :],
    )
    base_re, base_im = windowed(jnp.arange(C, dtype=jnp.int32), jnp.ones((F,), jnp.float32))
    q_re, q_im = project(
        mod_re.reshape(sub_cols * row_share, F),
        mod_im.reshape(sub_cols * row_share, F),
        base_re,
        base_im,
    )
    contrib = jnp.stack([q_re, q_im]).astype(jnp.bfloat16).reshape(2, sub_cols, row_share, C)
    arrived = lax.all_to_all(contrib, ("role", "grp"), split_axis=1, concat_axis=2, tiled=True)
    arrived = arrived.reshape(2, role_count, grp_count, row_share, C).astype(jnp.float32)
    quarter = jnp.sum(arrived, axis=1).astype(jnp.bfloat16)
    collected_rows = lax.all_gather(quarter[:, :, None], "rep", axis=2, tiled=True)
    subgrid = collected_rows.reshape(2, C, C)
    widened = extended(subgrid, ((("role", "grp"), 2),), EDGE)
    residual, regrid = degrid(
        widened, patch_pos[0], counts[0], vis_u[0], vis_v[0], observed[:, 0], kernel
    )
    left_part = regrid[:, :, :EDGE]
    right_part = regrid[:, :, EDGE + C :]
    center = regrid[:, :, EDGE : EDGE + C]
    from_right = shifted(left_part.astype(jnp.bfloat16), ("role", "grp"), -1).astype(
        left_part.dtype
    )
    from_left = shifted(right_part.astype(jnp.bfloat16), ("role", "grp"), 1).astype(
        right_part.dtype
    )
    resid = center.at[:, :, :EDGE].add(from_left).at[:, :, C - EDGE :].add(from_right)
    pieces = resid.reshape(2, grp_count * rep_count, row_share, C)
    spread = lax.all_to_all(
        pieces.astype(jnp.bfloat16), ("grp", "rep"), split_axis=1, concat_axis=1, tiled=True
    ).astype(pieces.dtype)
    owned = jnp.sum(spread.reshape(2, grp_count, rep_count, row_share, C), axis=2).astype(
        jnp.bfloat16
    )
    returned = lax.all_gather(owned, "role", axis=1, tiled=True)
    return (residual[:, None], returned)


LANES = 128
HALF = PATCH // 2
SLOTS = LANES // (2 * HALF)
TURN = 8
EVERYONE = ("role", "grp", "rep")


def lanes_of(shape):
    return lax.broadcasted_iota(jnp.int32, shape, len(shape) - 1)


def sublanes_of(shape):
    return lax.broadcasted_iota(jnp.int32, shape, len(shape) - 2)


def near(value):
    return pltpu.with_memory_space_constraint(value, pltpu.VMEM)


def far(value):
    return pltpu.with_memory_space_constraint(value, pltpu.HBM)


def waves(cells, scale):
    angles = np.arange(C)[:, None] * cells[None, :] % F * (2.0 * np.pi / F)
    return np.stack([np.cos(angles) * scale, np.sin(angles) * scale]).astype(np.float32)


def row_tables():
    cells = np.arange(LANES)
    return waves(cells, 1.0 / math.sqrt(F)), waves(np.full(LANES, LANES), 1.0)


def column_tables():
    cells = np.arange(LANES) % (LANES // 2) * TURN
    return waves(cells, 1.0 / math.sqrt(F)), waves(np.ones(LANES, np.int64), 1.0)


def eighth(index):
    def cosine(turn):
        turn = turn & 7
        size = jnp.where((turn & 1) == 1, math.sqrt(0.5), jnp.where((turn & 3) == 0, 1.0, 0.0))
        return jnp.where((turn > 2) & (turn < 6), -size, size).astype(jnp.float32)

    return cosine(index), cosine(index + 6)


def rotated(cos, sin, turn_cos, turn_sin):
    return cos * turn_cos - sin * turn_sin, sin * turn_cos + cos * turn_sin


def place_kernel(positions, place, copies):
    col_blocks = (C + 2 * EDGE) // PATCH
    slot = (lanes_of((1, LANES)) // HALF) % SLOTS
    value = jnp.zeros((1, LANES), jnp.int32)
    for p in range(SLOTS):
        value = jnp.where(slot == p, positions[0:1, p : p + 1], value)
    row = sum(jnp.where(value >= block * col_blocks, 1, 0) for block in range(1, C // PATCH))
    value = row * (8 - col_blocks) + value
    place[...] = value
    copies[...] = jnp.broadcast_to(value[None], copies.shape)


def row_kernel(
    rep_count, facets, taper_far, start_far, turn_far, keep, send, data, table_a, table_b,
    wave, turn, taper, total, strip, first_rows, second_rows, sems, small_sems,
):
    chunks, _, width = table_a.shape
    count = keep.shape[0]

    def fetch(chunk):
        columns = pl.ds(pl.multiple_of(chunk * width, width), width)
        return pltpu.make_async_copy(
            facets.at[0, :, :, columns], data.at[chunk], sems.at[chunk]
        )

    small = [
        pltpu.make_async_copy(source, target, small_sems.at[index])
        for index, (source, target) in enumerate(
            ((start_far, wave), (turn_far, turn), (taper_far, taper))
        )
    ]
    for copy in small:
        copy.start()
    fetch(0).start()
    total[...] = jnp.zeros_like(total)
    for copy in small:
        copy.wait()
    fetch(1).start()

    def build(step, carry):
        chunk, piece = step // (width // LANES), step % (width // LANES)
        window = taper[:, pl.ds(pl.multiple_of(step * LANES, LANES), LANES)]
        columns = pl.ds(pl.multiple_of(piece * LANES, LANES), LANES)
        for block in range(C // HALF):
            rows = slice(block * HALF, (block + 1) * HALF)
            cos, sin = wave[0, rows, :], wave[1, rows, :]
            re = window * cos
            im = window * sin
            base = (block % 2) * C + (block // 2) * HALF
            low = slice(base, base + HALF)
            high = slice(base + C // 2, base + C // 2 + HALF)
            table_a[chunk, low, columns] = re.astype(jnp.bfloat16)
            table_a[chunk, high, columns] = (-im).astype(jnp.bfloat16)
            table_b[chunk, low, columns] = im.astype(jnp.bfloat16)
            table_b[chunk, high, columns] = re.astype(jnp.bfloat16)
            cos, sin = rotated(cos, sin, turn[0, rows, :], turn[1, rows, :])
            wave[0, rows, :] = cos
            wave[1, rows, :] = sin
        return carry

    lax.fori_loop(0, chunks * (width // LANES), build, 0)

    def multiply(chunk, carry):
        fetch(chunk).wait()

        @pl.when(chunk + 2 < chunks)
        def _():
            fetch(chunk + 2).start()

        total[...] += contract(data[chunk, 0], table_a[chunk]) + contract(
            data[chunk, 1], table_b[chunk]
        )
        return carry

    lax.fori_loop(0, chunks, multiply, 0)
    place = lax.axis_index("grp") * rep_count + lax.axis_index("rep")
    for piece in range(count // LANES):
        offset = pl.multiple_of(place * count + piece * LANES, LANES)
        strip[piece : piece + 1, :] = taper[:, pl.ds(offset, LANES)]
    window = jnp.transpose(strip[...])
    for piece in range(count // LANES):
        rows = slice(piece * LANES, (piece + 1) * LANES)
        scaled = total[rows, :] * window[:, piece : piece + 1]
        first_rows[rows, :] = scaled[:, :C]
        second_rows[rows, :] = scaled[:, C:]
    even = lax.rem(lax.axis_index("rep"), 2) == 0
    part = count // TURN
    for turned in range(TURN):
        rows = pl.ds(turned, part, stride=TURN)
        first, second = first_rows[rows, :], second_rows[rows, :]
        target = slice(turned * part, (turned + 1) * part)
        keep[target, :] = jnp.where(even, first, second).astype(jnp.bfloat16)
        send[target, :] = jnp.where(even, second, first).astype(jnp.bfloat16)


def column_kernel(rep_count, keep, other, start, turn, sub, base, data, groups):
    part = keep.shape[0] // TURN
    mine = lax.axis_index("grp") * rep_count + lax.axis_index("rep")
    near_by = mine + 1 - 2 * lax.rem(mine, 2)
    shape = (HALF, LANES)
    right = lanes_of((1, LANES)) >= LANES // 2
    place = jnp.where(lanes_of(shape) < LANES // 2, mine, near_by)
    phase_cos, phase_sin = eighth((sublanes_of(shape) & 7) * place)
    for block in range(C // HALF):
        rows = slice(block * HALF, (block + 1) * HALF)
        cos, sin = rotated(start[0, rows, :], start[1, rows, :], phase_cos, phase_sin)
        for turned in range(TURN):
            base[turned, rows, :LANES] = cos.astype(jnp.bfloat16)
            base[turned, rows, LANES:] = sin.astype(jnp.bfloat16)
            if turned < TURN - 1:
                cos, sin = rotated(cos, sin, turn[0, rows, :], turn[1, rows, :])
    for turned in range(TURN):
        source = slice(turned * part, (turned + 1) * part)
        for side, ref in enumerate((keep, other)):
            value = ref[source, :]
            swapped = pltpu.roll(value.astype(jnp.float32), LANES // 2, 1)
            data[turned, side * part : (side + 1) * part, :] = value
            data[turned, (2 + side) * part : (3 + side) * part, :] = jnp.where(
                right, -swapped, swapped
            ).astype(jnp.bfloat16)
    for turned in range(TURN):
        groups[turned] = jnp.dot(base[turned], data[turned], preferred_element_type=jnp.float32)

    def quarter(value):
        swapped = pltpu.roll(value, LANES // 2, 1)
        return jnp.where(right, -swapped, swapped)

    def fourths(values):
        low, high = values[0] + values[2], values[0] - values[2]
        odd, turned = values[1] + values[3], quarter(values[1] - values[3])
        return low + odd, high + turned, low - odd, high - turned

    zero = jnp.zeros((EDGE, LANES), jnp.float32)
    sub[:EDGE, :] = zero
    sub[EDGE + TURN * C :, :] = zero
    size = math.sqrt(0.5)
    for block in range(C // HALF):
        rows = slice(block * HALF, (block + 1) * HALF)
        evens = fourths([groups[turned, rows, :] for turned in range(0, TURN, 2)])
        odds = fourths([groups[turned, rows, :] for turned in range(1, TURN, 2)])
        second, fourth = quarter(odds[1]), quarter(odds[3])
        twisted = (
            odds[0],
            (odds[1] + second) * size,
            quarter(odds[2]),
            (fourth - odds[3]) * size,
        )
        for column in range(TURN // 2):
            for sign in range(2):
                value = evens[column] - twisted[column] if sign else evens[column] + twisted[column]
                begin = EDGE + (column + sign * TURN // 2) * C + block * HALF
                sub[begin : begin + HALF, :] = value


def pack_kernel(rep_count, places, sub, out, spots, sem):
    copy = pltpu.make_async_copy(places, spots, sem)
    copy.start()
    copy.wait()
    slot = (lanes_of((1, LANES)) // HALF) % SLOTS

    def pack(column, carry):
        for rep in range(rep_count):
            device = column * rep_count + rep
            total = None
            for p in range(SLOTS):
                place = spots[device, 0, p * HALF]
                begin = pl.multiple_of(column * C + (place & 7) * PATCH, PATCH)
                block = sub[pl.ds(begin, PATCH), :]
                block = pltpu.roll(block, ((p - (place >> 3)) * HALF) & (LANES - 1), 1)
                total = block if total is None else jnp.where(slot == p, block, total)
            out[device] = total.astype(jnp.bfloat16)
        return carry

    lax.fori_loop(0, out.shape[0] // rep_count, pack, 0, unroll=2)


def degrid_kernel(
    counts, taps, place, arrived, observed, vis_u, vis_v, residual, out, taps_u, taps_v, weighted
):
    length = observed.shape[-1]
    left = lanes_of((PATCH, LANES)) < LANES // 2
    taps_u[...] = jnp.zeros_like(taps_u)

    def taps_of(offsets):
        distance = sublanes_of((PATCH, length)) - offsets
        value = jnp.zeros((PATCH, length), jnp.float32)
        for position in range(KW):
            value = jnp.where(distance == position, taps[position], value)
        return value

    for p in range(SLOTS):
        span = slice(p * length, (p + 1) * length)
        rows_u = taps_of(vis_u[0, p : p + 1, :])
        high = rows_u.astype(jnp.bfloat16)
        low = (rows_u - high.astype(jnp.float32)).astype(jnp.bfloat16)
        for half in range(2):
            begin = half * (LANES // 2) + p * HALF
            taps_u[begin : begin + HALF, span] = high[half * HALF : (half + 1) * HALF]
            taps_u[LANES + begin : LANES + begin + HALF, span] = low[
                half * HALF : (half + 1) * HALF
            ]
        taps_v[:, span] = taps_of(vis_v[0, p : p + 1, :])
    sums = []
    for half in range(2):
        total = arrived[half].astype(jnp.float32)
        for source in range(half + 2, arrived.shape[0], 2):
            total = total + arrived[source].astype(jnp.float32)
        sums.append(total)
    swapped = [pltpu.roll(total, LANES // 2, 1) for total in sums]
    patch = jnp.concatenate(
        [jnp.where(left, sums[0], swapped[1]), jnp.where(left, swapped[0], sums[1])], axis=0
    ).astype(jnp.bfloat16)
    patch = jnp.concatenate([patch, patch], axis=1)
    for p in range(SLOTS):
        span = slice(p * length, (p + 1) * length)
        inner = jnp.dot(patch, taps_u[:, span], preferred_element_type=jnp.float32)
        rows_v = taps_v[:, span]
        live = lanes_of((1, length)) < counts[0, p]
        for c in range(2):
            predicted = jnp.sum(inner[c * PATCH : (c + 1) * PATCH] * rows_v, axis=0, keepdims=True)
            value = jnp.where(live, observed[c, 0, p : p + 1, :] - predicted, 0.0)
            residual[c, 0, p : p + 1, :] = value
            value = value * rows_v
            high = value.astype(jnp.bfloat16)
            weighted[c * PATCH : (c + 1) * PATCH, span] = high
            weighted[2 * PATCH + c * PATCH : 2 * PATCH + (c + 1) * PATCH, span] = (
                value - high.astype(jnp.float32)
            ).astype(jnp.bfloat16)
    product = contract(weighted[...], taps_u[...])
    product = product[: 2 * PATCH] + product[2 * PATCH :]
    gridded = product[:, :LANES] + product[:, LANES:]
    parts = [gridded[:PATCH], gridded[PATCH:]]
    swapped = [pltpu.roll(part, LANES // 2, 1) for part in parts]
    halves = [jnp.where(left, parts[0], swapped[1]), jnp.where(left, swapped[0], parts[1])]
    row = place[...] >> 3
    owners = C // HALF
    for owner in range(owners):
        piece = jnp.where(row == owner // 2, halves[owner % 2], 0.0).astype(jnp.bfloat16)
        for first in range(0, out.shape[0], owners):
            out[first + owner] = piece


def return_kernel(rep_count, places, arrived, returned, canvas):
    sub_cols = returned.shape[1]
    col_blocks = (C + 2 * EDGE) // PATCH
    for column in range(sub_cols):
        values, marks = [], []
        for rep in range(rep_count):
            device = column * rep_count + rep
            values.append(arrived[device].astype(jnp.float32))
            marks.append(places[device] & 7)
        for block in range(col_blocks):
            total = jnp.where(marks[0] == block, values[0], 0.0)
            for value, mark in zip(values[1:], marks[1:]):
                total = total + jnp.where(mark == block, value, 0.0)
            canvas[column * col_blocks + block] = total
    shape = (2 * HALF, LANES)
    row, lane = sublanes_of(shape), lanes_of(shape)
    picked = (row // HALF == lane // (LANES // 2)) & (row % HALF == lane % HALF)
    pick = jnp.where(picked, 1.0, 0.0).astype(jnp.bfloat16)
    pick = jnp.concatenate([pick, pick], axis=1)
    for column in range(sub_cols):
        blocks = [canvas[column * col_blocks + 1 + block] for block in range(C // PATCH)]
        if column > 0:
            blocks[0] = blocks[0] + canvas[column * col_blocks - 1]
        if column < sub_cols - 1:
            blocks[-1] = blocks[-1] + canvas[(column + 1) * col_blocks]
        total = jnp.concatenate(blocks, axis=0)
        high = total.astype(jnp.bfloat16)
        low = (total - high.astype(jnp.float32)).astype(jnp.bfloat16)
        value = contract(pick, jnp.concatenate([high, low], axis=1)).astype(jnp.bfloat16)
        for c in range(2):
            returned[c, column] = value[c * HALF : (c + 1) * HALF]


def call(kernel, out_shape, operands, scratch, flops, scalars=0, far_operands=False, limit=24):
    spaces = [pltpu.SMEM] * scalars + [pltpu.VMEM] * (len(operands) - scalars)
    if far_operands:
        spaces = [pltpu.HBM] * len(operands)
    single = not isinstance(out_shape, tuple)
    spec = pl.BlockSpec(memory_space=pltpu.VMEM)
    return pl.pallas_call(
        kernel,
        out_shape=out_shape,
        in_specs=[pl.BlockSpec(memory_space=space) for space in spaces],
        out_specs=spec if single else (spec,) * len(out_shape),
        scratch_shapes=scratch,
        compiler_params=pltpu.CompilerParams(vmem_limit_bytes=limit << 20),
        cost_estimate=pl.CostEstimate(flops=flops, bytes_accessed=1 << 20, transcendentals=0),
    )(*operands)


def exchanged(value):
    return lax.all_to_all(value, EVERYONE, split_axis=0, concat_axis=0, tiled=True)


def fused(facets, taper, kernel, observed, patch_pos, counts, vis_u, vis_v):
    rep_count = lax.axis_size("rep")
    sub_cols = lax.axis_size("role") * lax.axis_size("grp")
    devices = sub_cols * rep_count
    count = facets.shape[2]
    length = observed.shape[-1]
    chunks = 4
    col_blocks = (C + 2 * EDGE) // PATCH
    f32, bf16 = jnp.float32, jnp.bfloat16

    place, copies = call(
        place_kernel,
        (pltpu.VMEM((1, LANES), jnp.int32), pltpu.VMEM((devices, 1, LANES), jnp.int32)),
        (patch_pos,),
        [],
        1 << 10,
    )
    places = exchanged(copies)
    places = near(places)
    strip = pltpu.VMEM((count, LANES), bf16)
    keep, send = call(
        lambda *refs: row_kernel(rep_count, *refs),
        (strip, strip),
        (far(facets), far(taper)) + tuple(far(jnp.asarray(table)) for table in row_tables()),
        [
            pltpu.VMEM((chunks, 2, count, F // chunks), bf16),
            pltpu.VMEM((chunks, 2 * C, F // chunks), bf16),
            pltpu.VMEM((chunks, 2 * C, F // chunks), bf16),
            pltpu.VMEM((2, C, LANES), f32),
            pltpu.VMEM((2, C, LANES), f32),
            pltpu.VMEM(taper.shape, f32),
            pltpu.VMEM((count, 2 * C), f32),
            pltpu.VMEM((8, LANES), f32),
            pltpu.VMEM((count, LANES), f32),
            pltpu.VMEM((count, LANES), f32),
            pltpu.SemaphoreType.DMA((chunks,)),
            pltpu.SemaphoreType.DMA((3,)),
        ],
        8 * C * F * count,
        far_operands=True,
    )
    pairs = [(i, i + 1 - 2 * (i % 2)) for i in range(rep_count)]
    other = near(lax.ppermute(send, "rep", pairs))
    sub = call(
        lambda *refs: column_kernel(rep_count, *refs),
        pltpu.VMEM((sub_cols * C + 2 * EDGE, LANES), f32),
        (near(keep), other) + tuple(near(table) for table in column_tables()),
        [
            pltpu.VMEM((TURN, C, 2 * LANES), bf16),
            pltpu.VMEM((TURN, 2 * LANES, LANES), bf16),
            pltpu.VMEM((TURN, C, LANES), f32),
        ],
        1 << 20,
    )
    chunk = pltpu.VMEM((devices, PATCH, LANES), bf16)
    outgoing = call(
        lambda *refs: pack_kernel(rep_count, *refs),
        chunk,
        (places, near(sub)),
        [pltpu.SMEM((devices, 1, LANES), jnp.int32), pltpu.SemaphoreType.DMA],
        1 << 28,
    )
    arrived = near(exchanged(outgoing))
    residual, gridded = call(
        degrid_kernel,
        (jax.ShapeDtypeStruct(observed.shape, f32), chunk),
        (counts, kernel, place, arrived, near(observed), near(vis_u), near(vis_v)),
        [
            pltpu.VMEM((2 * LANES, SLOTS * length), bf16),
            pltpu.VMEM((PATCH, SLOTS * length), f32),
            pltpu.VMEM((4 * PATCH, SLOTS * length), bf16),
        ],
        1 << 28,
        scalars=2,
    )
    spread = near(exchanged(gridded))
    returned = call(
        lambda *refs: return_kernel(rep_count, *refs),
        jax.ShapeDtypeStruct((2, sub_cols, HALF, C), bf16),
        (places, spread),
        [pltpu.VMEM((sub_cols * col_blocks, PATCH, LANES), f32)],
        1 << 26,
    )
    return (residual, returned)


def part(facets, taper, kernel, observed, patch_pos, counts, vis_u, vis_v):
    grp_count = lax.axis_size("grp")
    rep_count = lax.axis_size("rep")
    owners = grp_count * rep_count
    sub_cols = lax.axis_size("role") * grp_count
    whole = (
        owners * HALF == C
        and owners == TURN
        and sub_cols == TURN
        and facets.shape[2] * TURN == F
        and rep_count % 2 == 0
        and patch_pos.shape[1] == SLOTS
        and facets.shape[2] == TURN * LANES // 2
        and observed.shape[-1] % LANES == 0
    )
    path = fused if whole else local
    return path(facets, taper, kernel, observed, patch_pos, counts, vis_u, vis_v)


def solution(mesh):
    return jax.shard_map(
        part,
        mesh=mesh,
        in_specs=(
            P("role", None, ("grp", "rep"), None),
            P("role", None),
            P(),
            P(None, ("role", "grp"), "rep", None),
            P(("role", "grp"), "rep"),
            P(("role", "grp"), "rep"),
            P(("role", "grp"), "rep", None),
            P(("role", "grp"), "rep", None),
        ),
        out_specs=(P(None, ("role", "grp"), "rep", None), P(None, None, ("grp", "rep"), None)),
        check_vma=False,
    )
```

profile of v0, /device:TPU:0, one launch (start us, length us, event | category | flops | bytes accessed | tf_op | source)
XLA Modules:
  0.0 51.6 jit_solution(14255960491096001213)
XLA Ops:
  0.6 0.0 copy-start
  0.6 0.0 copy-start.1
  0.7 0.0 copy-start.5
  0.7 0.0 copy-start.4
  0.7 0.0 copy-start.3
  0.7 0.0 copy-start.6
  0.7 0.0 copy-start.2
  0.7 0.0 copy-start.7
  0.7 6.3 %shard_map.132 = (bf16[512,128]{1,0:T(8,128)(2,1)S(1)}, bf16[512,128]{1,0:T(8,128)(2,1)S(1)}) custom-call(bf16[1,2,512,4096]{3,2,1,0:T(8,128)(2,1)} %refs_0_.1, f32[1,4096]{1,0:T(1,128)} %refs_1_.1, f32[2,128,128]{2,1,0:T(8,128)} %constant.8.clone.refs_2_, f32[2,128,128]{2,1,0:T(8,128)} %constant.9.clone.refs_3_), custom_call_target="tpu_custom_call" | custom-call | flops 2147483648 | bytes 1048576 | tf_op jit(solution)/shard_map/pallas_call | solution.py:499
  7.0 0.6 %collective-permute-start = (bf16[512,128]{1,0:T(8,128)(2,1)S(1)}, bf16[512,128]{1,0:T(8,128)(2,1)S(1)}, u32[]{:S(2)}, u32[]{:S(2)}) collective-permute-start(bf16[512,128]{1,0:T(8,128)(2,1)S(1)} %get-tuple-element.11), channel_id=1, source_target_pairs={{0,1},{1,0},{2,3},{3,2},{4,5},{5,4},{6,7},{7,6},{8,9},{9,8},{10,11... | collective-permute-start | bytes 393224 | tf_op jit(solution)/shard_map/ppermute | solution.py:556
  7.6 0.0 copy-done.5
  7.6 0.7 %shard_map.131 = (s32[1,128]{1,0:T(1,128)S(1)}, s32[32,1,128]{2,1,0:T(1,128)}) custom-call(s32[1,4]{1,0:T(1,128)S(1)} %copy-done.5), custom_call_target="tpu_custom_call" | custom-call | flops 1024 | bytes 1048576 | tf_op jit(solution)/shard_map/pallas_call | solution.py:499
  8.3 6.9 %all-to-all-start = ((s32[32,1,128]{2,1,0:T(1,128)}), s32[32,1,128]{2,1,0:T(1,128)S(1)}, u32[]{:S(2)}, u32[]{:S(2)}) async-start(s32[32,1,128]{2,1,0:T(1,128)} %get-tuple-element.9), calls=%async_computation | async-start | bytes 32768 | tf_op jit(solution)/shard_map/all_to_all | solution.py:511
  15.3 0.0 collective-permute-done.refs_1_
  15.3 0.0 copy-done
  15.3 0.0 copy-done.1
  15.3 0.6 %shard_map.133.refs_1_ = f32[1088,128]{1,0:T(8,128)S(1)} custom-call(bf16[512,128]{1,0:T(8,128)(2,1)S(1)} %get-tuple-element.10.refs_0_, bf16[512,128]{1,0:T(8,128)(2,1)S(1)} %collective-permute-done.refs_1_, f32[2,128,128]{2,1,0:T(8,128)S(1)} %copy-done.1, f32[2,128,128]{2,1,0:T(8,128)S(1)} %copy-done), custom_call_target="tpu_custom_call" | custom-call | flops 1048576 | bytes 1048576 | tf_op jit(solution)/shard_map/pallas_call | solution.py:499
  15.9 6.5 %all-to-all-done.refs_0_ = s32[32,1,128]{2,1,0:T(1,128)S(1)} async-done(((s32[32,1,128]{2,1,0:T(1,128)}), s32[32,1,128]{2,1,0:T(1,128)S(1)}, u32[]{:S(2)}, u32[]{:S(2)}) %all-to-all-start) | async-done | bytes 16416 | tf_op jit(solution)/shard_map/all_to_all | solution.py:511
  22.4 1.4 %shard_map.134 = bf16[32,32,128]{2,1,0:T(8,128)(2,1)S(1)} custom-call(s32[32,1,128]{2,1,0:T(1,128)S(1)} %all-to-all-done.refs_0_, f32[1088,128]{1,0:T(8,128)S(1)} %shard_map.133.refs_1_), custom_call_target="tpu_custom_call" | custom-call | flops 268435456 | bytes 1048576 | tf_op jit(solution)/shard_map/pallas_call | solution.py:499
  23.8 12.3 %all_to_all.15.arrived = bf16[32,32,128]{2,1,0:T(8,128)(2,1)S(1)} all-to-all(bf16[32,32,128]{2,1,0:T(8,128)(2,1)S(1)} %shard_map.134), channel_id=1, replica_groups=mesh['role'=4,'grp'=2,'rep'=4] {'role','grp','rep'}, dimensions={0} | all-to-all | bytes 524288 | tf_op jit(solution)/shard_map/all_to_all | solution.py:511
  36.1 0.0 copy-done.4
  36.1 0.0 copy-done.3
  36.1 0.0 copy-done.6
  36.1 0.0 copy-done.2
  36.1 0.0 copy-done.7
  36.1 1.7 %shard_map.135 = (f32[2,1,4,512]{3,2,1,0:T(4,128)}, bf16[32,32,128]{2,1,0:T(8,128)(2,1)S(1)}) custom-call(s32[1,4]{1,0:T(1,128)S(1)} %copy-done.6, f32[8]{0:T(128)S(1)} %copy-done.7, s32[1,128]{1,0:T(1,128)S(1)} %get-tuple-element.8.place, bf16[32,32,128]{2,1,0:T(8,128)(2,1)S(1)} %all_to_all.15.arrived, f32[2,1,4,512]{3,2,1,0:T(4,128)S(1)} %copy-done.2, ...), custom_call_target="tpu_custom_call" | custom-call | flops 268435456 | bytes 1048576 | tf_op jit(solution)/shard_map/pallas_call | solution.py:499
  37.8 12.7 %all_to_all.16.refs_1_ = bf16[32,32,128]{2,1,0:T(8,128)(2,1)S(1)} all-to-all(bf16[32,32,128]{2,1,0:T(8,128)(2,1)S(1)} %get-tuple-element.13), channel_id=1, replica_groups=mesh['role'=4,'grp'=2,'rep'=4] {'role','grp','rep'}, dimensions={0} | all-to-all | bytes 524288 | tf_op jit(solution)/shard_map/all_to_all | solution.py:511
  50.5 1.1 %shard_map.136 = bf16[2,8,16,128]{3,2,1,0:T(8,128)(2,1)} custom-call(s32[32,1,128]{2,1,0:T(1,128)S(1)} %all-to-all-done.refs_0_, bf16[32,32,128]{2,1,0:T(8,128)(2,1)S(1)} %all_to_all.16.refs_1_), custom_call_target="tpu_custom_call" | custom-call | flops 67108864 | bytes 1048576 | tf_op jit(solution)/shard_map/pallas_call | solution.py:499
Async XLA Ops:
  0.6 14.6 %copy-start = (f32[2,128,128]{2,1,0:T(8,128)S(1)}, f32[2,128,128]{2,1,0:T(8,128)}, u32[]{:S(2)}) copy-start(f32[2,128,128]{2,1,0:T(8,128)} %constant.11.clone.refs_3_) | copy-start | bytes 393220
  0.6 14.6 %copy-start.1 = (f32[2,128,128]{2,1,0:T(8,128)S(1)}, f32[2,128,128]{2,1,0:T(8,128)}, u32[]{:S(2)}) copy-start(f32[2,128,128]{2,1,0:T(8,128)} %constant.10.clone.refs_2_) | copy-start | bytes 393220
  0.7 6.9 %copy-start.5 = (s32[1,4]{1,0:T(1,128)S(1)}, s32[1,4]{1,0:T(1,128)}, u32[]{:S(2)}) copy-start(s32[1,4]{1,0:T(1,128)} %positions.1) | copy-start | bytes 52
  0.7 35.4 %copy-start.4 = (s32[1,4,512]{2,1,0:T(4,128)S(1)}, s32[1,4,512]{2,1,0:T(4,128)}, u32[]{:S(2)}) copy-start(s32[1,4,512]{2,1,0:T(4,128)} %vis_v.1) | copy-start | bytes 24580
  0.7 35.4 %copy-start.3 = (s32[1,4,512]{2,1,0:T(4,128)S(1)}, s32[1,4,512]{2,1,0:T(4,128)}, u32[]{:S(2)}) copy-start(s32[1,4,512]{2,1,0:T(4,128)} %vis_u.1) | copy-start | bytes 24580
  0.7 35.4 %copy-start.6 = (s32[1,4]{1,0:T(1,128)S(1)}, s32[1,4]{1,0:T(1,128)}, u32[]{:S(2)}) copy-start(s32[1,4]{1,0:T(1,128)} %counts.1) | copy-start | bytes 52
  0.7 35.4 %copy-start.2 = (f32[2,1,4,512]{3,2,1,0:T(4,128)S(1)}, f32[2,1,4,512]{3,2,1,0:T(4,128)}, u32[]{:S(2)}) copy-start(f32[2,1,4,512]{3,2,1,0:T(4,128)} %observed.1) | copy-start | bytes 49156
  0.7 35.4 %copy-start.7 = (f32[8]{0:T(128)S(1)}, f32[8]{0:T(128)}, u32[]{:S(2)}) copy-start(f32[8]{0:T(128)} %taps.1) | copy-start | bytes 100
  7.0 8.2 %collective-permute-start = (bf16[512,128]{1,0:T(8,128)(2,1)S(1)}, bf16[512,128]{1,0:T(8,128)(2,1)S(1)}, u32[]{:S(2)}, u32[]{:S(2)}) collective-permute-start(bf16[512,128]{1,0:T(8,128)(2,1)S(1)} %get-tuple-element.11), channel_id=1, source_target_pairs={{0,1},{1,0},{2,3},{3,2},{4,5},{5,4},{6,7},{7,6},{8,9},{9,8},{10,11... | collective-permute-start | bytes 393224 | tf_op jit(solution)/shard_map/ppermute | solution.py:556
  8.3 14.1 %all-to-all-start = ((s32[32,1,128]{2,1,0:T(1,128)}), s32[32,1,128]{2,1,0:T(1,128)S(1)}, u32[]{:S(2)}, u32[]{:S(2)}) async-start(s32[32,1,128]{2,1,0:T(1,128)} %get-tuple-element.9), calls=%async_computation | async-start | bytes 32768 | tf_op jit(solution)/shard_map/all_to_all | solution.py:511
where the time goes:
time: 51.9 us; the launch traced here: 51.6 us
  blocking collectives  25 us (48%)
  Pallas kernels  11.9 us (23%)
  starting transfers between devices  7.5 us (14%)
  waiting for transfers between devices  6.48 us (12%)
  between operations  0.77 us (1%)
    all_to_all x2, blocking collectives, exchanged(): lax.all_to_all(value, EVERYONE, split_axis=0, concat_axis=0, tiled=True)  25 us
    pallas_call x6, Pallas kernels, call(): pl.pallas_call(kernel, out_shape=out_shape, in_specs=[pl.BlockSpec(memory...  11.9 us
    all_to_all x1, starting transfers between devices, exchanged(): lax.all_to_all(value, EVERYONE, split_axis=0, concat_axis=0, tiled=True)  6.95 us
    all_to_all x1, waiting for transfers between devices, exchanged(): lax.all_to_all(value, EVERYONE, split_axis=0, concat_axis=0, tiled=True)  6.48 us
  transfers between devices with their start and end apart: 2, of which 1 were waited for; matrix products, arithmetic and copies ran while one was open for 0% of the time, Pallas kernels for 2%

commit v1 on v0

--- a/solution.py
+++ b/solution.py
@@ -228,8 +228,8 @@
 
 
 def row_kernel(
-    rep_count, facets, taper_far, start_far, turn_far, keep, send, data, table_a, table_b,
-    wave, turn, taper, total, strip, first_rows, second_rows, sems, small_sems,
+    rep_count, facets, taper, start, turn, keep, send, data, table_a, table_b,
+    wave, total, strip, first_rows, second_rows, sems,
 ):
     chunks, _, width = table_a.shape
     count = keep.shape[0]
@@ -240,19 +240,10 @@
             facets.at[0, :, :, columns], data.at[chunk], sems.at[chunk]
         )
 
-    small = [
-        pltpu.make_async_copy(source, target, small_sems.at[index])
-        for index, (source, target) in enumerate(
-            ((start_far, wave), (turn_far, turn), (taper_far, taper))
-        )
-    ]
-    for copy in small:
-        copy.start()
     fetch(0).start()
+    fetch(1).start()
+    wave[...] = start[...]
     total[...] = jnp.zeros_like(total)
-    for copy in small:
-        copy.wait()
-    fetch(1).start()
 
     def build(step, carry):
         chunk, piece = step // (width // LANES), step % (width // LANES)
@@ -369,33 +360,29 @@
                 sub[begin : begin + HALF, :] = value
 
 
-def pack_kernel(rep_count, places, sub, out, spots, sem):
-    copy = pltpu.make_async_copy(places, spots, sem)
-    copy.start()
-    copy.wait()
-    slot = (lanes_of((1, LANES)) // HALF) % SLOTS
+def pack_kernel(rep_count, places, sub, out):
+    col_blocks = (C + 2 * EDGE) // PATCH
+    lane = lanes_of((PATCH, LANES))
+    fixed = lane - (lane // HALF) % SLOTS * HALF
 
     def pack(column, carry):
+        begin = pl.multiple_of(column * C, C)
+        blocks = [sub[pl.ds(begin + block * PATCH, PATCH), :] for block in range(col_blocks)]
         for rep in range(rep_count):
-            device = column * rep_count + rep
-            total = None
-            for p in range(SLOTS):
-                place = spots[device, 0, p * HALF]
-                begin = pl.multiple_of(column * C + (place & 7) * PATCH, PATCH)
-                block = sub[pl.ds(begin, PATCH), :]
-                block = pltpu.roll(block, ((p - (place >> 3)) * HALF) & (LANES - 1), 1)
-                total = block if total is None else jnp.where(slot == p, block, total)
-            out[device] = total.astype(jnp.bfloat16)
+            mark = jnp.broadcast_to(places[column * rep_count + rep], (PATCH, LANES))
+            source, wanted = fixed + (mark >> 3) * HALF, mark & 7
+            total = jnp.zeros((PATCH, LANES), jnp.float32)
+            for block in range(col_blocks):
+                moved = jnp.take_along_axis(blocks[block], source, axis=1)
+                total = jnp.where(wanted == block, moved, total)
+            out[column * rep_count + rep] = total.astype(jnp.bfloat16)
         return carry
 
-    lax.fori_loop(0, out.shape[0] // rep_count, pack, 0, unroll=2)
-
-
-def degrid_kernel(
-    counts, taps, place, arrived, observed, vis_u, vis_v, residual, out, taps_u, taps_v, weighted
-):
-    length = observed.shape[-1]
-    left = lanes_of((PATCH, LANES)) < LANES // 2
+    lax.fori_loop(0, out.shape[0] // rep_count, pack, 0, unroll=True)
+
+
+def taps_kernel(taps, vis_u, vis_v, taps_u, taps_v):
+    length = vis_u.shape[-1]
     taps_u[...] = jnp.zeros_like(taps_u)
 
     def taps_of(offsets):
@@ -417,6 +404,13 @@
                 half * HALF : (half + 1) * HALF
             ]
         taps_v[:, span] = taps_of(vis_v[0, p : p + 1, :])
+
+
+def degrid_kernel(
+    counts, place, arrived, observed, taps_u, taps_v, residual_far, out, weighted, residual, sem
+):
+    length = observed.shape[-1]
+    left = lanes_of((PATCH, LANES)) < LANES // 2
     sums = []
     for half in range(2):
         total = arrived[half].astype(jnp.float32)
@@ -432,7 +426,7 @@
         span = slice(p * length, (p + 1) * length)
         inner = jnp.dot(patch, taps_u[:, span], preferred_element_type=jnp.float32)
         rows_v = taps_v[:, span]
-        live = lanes_of((1, length)) < counts[0, p]
+        live = lanes_of((1, length)) < counts[0:1, p : p + 1]
         for c in range(2):
             predicted = jnp.sum(inner[c * PATCH : (c + 1) * PATCH] * rows_v, axis=0, keepdims=True)
             value = jnp.where(live, observed[c, 0, p : p + 1, :] - predicted, 0.0)
@@ -443,6 +437,8 @@
             weighted[2 * PATCH + c * PATCH : 2 * PATCH + (c + 1) * PATCH, span] = (
                 value - high.astype(jnp.float32)
             ).astype(jnp.bfloat16)
+    copy = pltpu.make_async_copy(residual, residual_far, sem)
+    copy.start()
     product = contract(weighted[...], taps_u[...])
     product = product[: 2 * PATCH] + product[2 * PATCH :]
     gridded = product[:, :LANES] + product[:, LANES:]
@@ -455,6 +451,7 @@
         piece = jnp.where(row == owner // 2, halves[owner % 2], 0.0).astype(jnp.bfloat16)
         for first in range(0, out.shape[0], owners):
             out[first + owner] = piece
+    copy.wait()
 
 
 def return_kernel(rep_count, places, arrived, returned, canvas):
@@ -490,17 +487,18 @@
             returned[c, column] = value[c * HALF : (c + 1) * HALF]
 
 
-def call(kernel, out_shape, operands, scratch, flops, scalars=0, far_operands=False, limit=24):
+def call(kernel, out_shape, operands, scratch, flops, scalars=0, first=None, outs=None, limit=24):
     spaces = [pltpu.SMEM] * scalars + [pltpu.VMEM] * (len(operands) - scalars)
-    if far_operands:
-        spaces = [pltpu.HBM] * len(operands)
+    if first is not None:
+        spaces[0] = first
     single = not isinstance(out_shape, tuple)
-    spec = pl.BlockSpec(memory_space=pltpu.VMEM)
+    outs = outs or (pltpu.VMEM,) * (1 if single else len(out_shape))
+    specs = tuple(pl.BlockSpec(memory_space=space) for space in outs)
     return pl.pallas_call(
         kernel,
         out_shape=out_shape,
         in_specs=[pl.BlockSpec(memory_space=space) for space in spaces],
-        out_specs=spec if single else (spec,) * len(out_shape),
+        out_specs=specs[0] if single else specs,
         scratch_shapes=scratch,
         compiler_params=pltpu.CompilerParams(vmem_limit_bytes=limit << 20),
         cost_estimate=pl.CostEstimate(flops=flops, bytes_accessed=1 << 20, transcendentals=0),
@@ -526,7 +524,7 @@
         (pltpu.VMEM((1, LANES), jnp.int32), pltpu.VMEM((devices, 1, LANES), jnp.int32)),
         (patch_pos,),
         [],
-        1 << 10,
+        1 << 33,
     )
     places = exchanged(copies)
     places = near(places)
@@ -534,26 +532,35 @@
     keep, send = call(
         lambda *refs: row_kernel(rep_count, *refs),
         (strip, strip),
-        (far(facets), far(taper)) + tuple(far(jnp.asarray(table)) for table in row_tables()),
+        (far(facets), near(taper)) + tuple(near(jnp.asarray(table)) for table in row_tables()),
         [
             pltpu.VMEM((chunks, 2, count, F // chunks), bf16),
             pltpu.VMEM((chunks, 2 * C, F // chunks), bf16),
             pltpu.VMEM((chunks, 2 * C, F // chunks), bf16),
             pltpu.VMEM((2, C, LANES), f32),
-            pltpu.VMEM((2, C, LANES), f32),
-            pltpu.VMEM(taper.shape, f32),
             pltpu.VMEM((count, 2 * C), f32),
             pltpu.VMEM((8, LANES), f32),
             pltpu.VMEM((count, LANES), f32),
             pltpu.VMEM((count, LANES), f32),
             pltpu.SemaphoreType.DMA((chunks,)),
-            pltpu.SemaphoreType.DMA((3,)),
         ],
         8 * C * F * count,
-        far_operands=True,
+        first=pltpu.HBM,
     )
     pairs = [(i, i + 1 - 2 * (i % 2)) for i in range(rep_count)]
-    other = near(lax.ppermute(send, "rep", pairs))
+    other = lax.ppermute(send, "rep", pairs)
+    other = near(other)
+    taps_u, taps_v = call(
+        taps_kernel,
+        (
+            pltpu.VMEM((2 * LANES, SLOTS * length), bf16),
+            pltpu.VMEM((PATCH, SLOTS * length), f32),
+        ),
+        (kernel, near(vis_u), near(vis_v)),
+        [],
+        1 << 26,
+        scalars=1,
+    )
     sub = call(
         lambda *refs: column_kernel(rep_count, *refs),
         pltpu.VMEM((sub_cols * C + 2 * EDGE, LANES), f32),
@@ -567,24 +574,20 @@
     )
     chunk = pltpu.VMEM((devices, PATCH, LANES), bf16)
     outgoing = call(
-        lambda *refs: pack_kernel(rep_count, *refs),
-        chunk,
-        (places, near(sub)),
-        [pltpu.SMEM((devices, 1, LANES), jnp.int32), pltpu.SemaphoreType.DMA],
-        1 << 28,
+        lambda *refs: pack_kernel(rep_count, *refs), chunk, (places, near(sub)), [], 1 << 28
     )
     arrived = near(exchanged(outgoing))
     residual, gridded = call(
         degrid_kernel,
-        (jax.ShapeDtypeStruct(observed.shape, f32), chunk),
-        (counts, kernel, place, arrived, near(observed), near(vis_u), near(vis_v)),
+        (pltpu.HBM(observed.shape, f32), chunk),
+        (near(counts), place, arrived, near(observed), near(taps_u), near(taps_v)),
         [
-            pltpu.VMEM((2 * LANES, SLOTS * length), bf16),
-            pltpu.VMEM((PATCH, SLOTS * length), f32),
             pltpu.VMEM((4 * PATCH, SLOTS * length), bf16),
+            pltpu.VMEM(observed.shape, f32),
+            pltpu.SemaphoreType.DMA,
         ],
         1 << 28,
-        scalars=2,
+        outs=(pltpu.HBM, pltpu.VMEM),
     )
     spread = near(exchanged(gridded))
     returned = call(

time: 51.9 us -> 53.6 us (1.033)
  blocking collectives: 25 us -> 12.7 us
  waiting for transfers between devices: 6.48 us -> 16.1 us
  starting transfers between devices: 7.5 us -> 10.1 us
  local copies, waits for them, and re-layouts: 0.04 us -> 2.57 us
  Pallas kernels: 11.9 us -> 10.9 us
    all_to_all x2 -> x1, blocking collectives: 25 us -> 12.7 us  [exchanged(): lax.all_to_all(value, EVERYONE, split_axis=0, concat_axis=0, tiled=True)]
    all_to_all x1 -> x2, waiting for transfers between devices: 6.48 us -> 16.1 us  [exchanged(): lax.all_to_all(value, EVERYONE, split_axis=0, concat_axis=0, tiled=True)]
    all_to_all x1 -> x2, starting transfers between devices: 6.95 us -> 9.54 us  [exchanged(): lax.all_to_all(value, EVERYONE, split_axis=0, concat_axis=0, tiled=True)]
    unnamed x16 -> x22, local copies, waits for them, and re-layouts: 0.04 us -> 2.57 us
    pallas_call x6 -> x7, Pallas kernels: 11.9 us -> 10.9 us  [call(): pl.pallas_call(kernel, out_shape=out_shape, in_specs=[pl.BlockSpec(memory...]
  transfers between devices with their start and end apart: 2 -> 3, of which waited for: 1 -> 2; matrix products, arithmetic and copies ran while one was open for 0% -> 0% of each run, Pallas kernels for 2% -> 4%
where the time goes in v1:
time: 53.6 us; the launch traced here: 53.2 us
  waiting for transfers between devices  16.1 us (30%)
  blocking collectives  12.7 us (24%)
  Pallas kernels  10.9 us (20%)
  starting transfers between devices  10.1 us (19%)
  local copies, waits for them, and re-layouts  2.57 us (5%)
  between operations  0.8 us (1%)
    all_to_all x2, waiting for transfers between devices, exchanged(): lax.all_to_all(value, EVERYONE, split_axis=0, concat_axis=0, tiled=True)  16.1 us
    all_to_all x1, blocking collectives, exchanged(): lax.all_to_all(value, EVERYONE, split_axis=0, concat_axis=0, tiled=True)  12.7 us
    pallas_call x7, Pallas kernels, call(): pl.pallas_call(kernel, out_shape=out_shape, in_specs=[pl.BlockSpec(memory...  10.9 us
    all_to_all x2, starting transfers between devices, exchanged(): lax.all_to_all(value, EVERYONE, split_axis=0, concat_axis=0, tiled=True)  9.54 us
    unnamed x22, local copies, waits for them, and re-layouts  2.57 us
  transfers between devices with their start and end apart: 3, of which 2 were waited for; matrix products, arithmetic and copies ran while one was open for 0% of the time, Pallas kernels for 4%

profile of v1, /device:TPU:0, one launch (start us, length us, event | category | flops | bytes accessed | tf_op | source)
XLA Modules:
  0.0 53.2 jit_solution(11809731094935603944)
XLA Ops:
  0.6 0.0 copy-start
  0.6 0.9 %copy-done = f32[2,128,128]{2,1,0:T(8,128)S(1)} copy-done((f32[2,128,128]{2,1,0:T(8,128)S(1)}, f32[2,128,128]{2,1,0:T(8,128)}, u32[]{:S(2)}) %copy-start) | copy-done | bytes 131096
  1.5 0.9 %copy-done.1 = f32[2,128,128]{2,1,0:T(8,128)S(1)} copy-done((f32[2,128,128]{2,1,0:T(8,128)S(1)}, f32[2,128,128]{2,1,0:T(8,128)}, u32[]{:S(2)}) %copy-start.1) | copy-done | bytes 131096
  2.4 0.7 %copy-done.4 = f32[1,4096]{1,0:T(1,128)S(1)} copy-done((f32[1,4096]{1,0:T(1,128)S(1)}, f32[1,4096]{1,0:T(1,128)}, u32[]{:S(2)}) %copy-start.4) | copy-done | bytes 16408
  3.2 5.2 %shard_map.132 = (bf16[512,128]{1,0:T(8,128)(2,1)S(1)}, bf16[512,128]{1,0:T(8,128)(2,1)S(1)}) custom-call(bf16[1,2,512,4096]{3,2,1,0:T(8,128)(2,1)} %refs_0_.1, f32[1,4096]{1,0:T(1,128)S(1)} %copy-done.4, f32[2,128,128]{2,1,0:T(8,128)S(1)} %copy-done.1, f32[2,128,128]{2,1,0:T(8,128)S(1)} %copy-done), custom_call_target="tpu_custom_call" | custom-call | flops 2147483648 | bytes 1048576 | tf_op jit(solution)/shard_map/pallas_call | solution.py:497
  8.4 0.0 copy-start.2
  8.4 0.0 copy-start.3
  8.4 0.0 copy-start.7
  8.4 0.0 copy-start.8
  8.4 0.0 copy-start.10
  8.4 0.0 copy-start.5
  8.5 0.0 copy-start.6
  8.5 0.6 %collective-permute-start = (bf16[512,128]{1,0:T(8,128)(2,1)S(1)}, bf16[512,128]{1,0:T(8,128)(2,1)S(1)}, u32[]{:S(2)}, u32[]{:S(2)}) collective-permute-start(bf16[512,128]{1,0:T(8,128)(2,1)S(1)} %get-tuple-element.13), channel_id=1, source_target_pairs={{0,1},{1,0},{2,3},{3,2},{4,5},{5,4},{6,7},{7,6},{8,9},{9,8},{10,11... | collective-permute-start | bytes 393224 | tf_op jit(solution)/shard_map/ppermute | solution.py:551
  9.0 0.0 copy-done.9
  9.0 0.7 %shard_map.131 = (s32[1,128]{1,0:T(1,128)S(1)}, s32[32,1,128]{2,1,0:T(1,128)}) custom-call(s32[1,4]{1,0:T(1,128)S(1)} %copy-done.9), custom_call_target="tpu_custom_call" | custom-call | flops 8589934592 | bytes 1048576 | tf_op jit(solution)/shard_map/pallas_call | solution.py:497
  9.7 7.0 %all-to-all-start = ((s32[32,1,128]{2,1,0:T(1,128)}), s32[32,1,128]{2,1,0:T(1,128)S(1)}, u32[]{:S(2)}, u32[]{:S(2)}) async-start(s32[32,1,128]{2,1,0:T(1,128)} %get-tuple-element.11), calls=%async_computation | async-start | bytes 32768 | tf_op jit(solution)/shard_map/all_to_all | solution.py:509
  16.7 0.0 collective-permute-done.refs_1_
  16.7 0.0 copy-done.2
  16.7 0.0 copy-done.3
  16.7 0.6 %shard_map.133.refs_1_ = f32[1088,128]{1,0:T(8,128)S(1)} custom-call(bf16[512,128]{1,0:T(8,128)(2,1)S(1)} %get-tuple-element.12.refs_0_, bf16[512,128]{1,0:T(8,128)(2,1)S(1)} %collective-permute-done.refs_1_, f32[2,128,128]{2,1,0:T(8,128)S(1)} %copy-done.3, f32[2,128,128]{2,1,0:T(8,128)S(1)} %copy-done.2), custom_call_target="tpu_custom_call" | custom-call | flops 1048576 | bytes 1048576 | tf_op jit(solution)/shard_map/pallas_call | solution.py:497
  17.3 6.5 %all-to-all-done.refs_0_ = s32[32,1,128]{2,1,0:T(1,128)S(1)} async-done(((s32[32,1,128]{2,1,0:T(1,128)}), s32[32,1,128]{2,1,0:T(1,128)S(1)}, u32[]{:S(2)}, u32[]{:S(2)}) %all-to-all-start) | async-done | bytes 16416 | tf_op jit(solution)/shard_map/all_to_all | solution.py:509
  23.8 1.3 %shard_map.134 = bf16[32,32,128]{2,1,0:T(8,128)(2,1)} custom-call(s32[32,1,128]{2,1,0:T(1,128)S(1)} %all-to-all-done.refs_0_, f32[1088,128]{1,0:T(8,128)S(1)} %shard_map.133.refs_1_), custom_call_target="tpu_custom_call" | custom-call | flops 268435456 | bytes 1048576 | tf_op jit(solution)/shard_map/pallas_call | solution.py:497
  25.1 2.6 %all-to-all-start.1 = ((bf16[32,32,128]{2,1,0:T(8,128)(2,1)}), bf16[32,32,128]{2,1,0:T(8,128)(2,1)S(1)}, u32[]{:S(2)}, u32[]{:S(2)}) async-start(bf16[32,32,128]{2,1,0:T(8,128)(2,1)} %shard_map.134), calls=%async_computation.1 | async-start | bytes 524288 | tf_op jit(solution)/shard_map/all_to_all | solution.py:509
  27.7 0.0 copy-done.7
  27.7 0.0 copy-done.8
  27.7 0.0 copy-done.10
  27.7 0.9 %shard_map.135 = (bf16[256,2048]{1,0:T(8,128)(2,1)S(1)}, f32[32,2048]{1,0:T(8,128)S(1)}) custom-call(f32[8]{0:T(128)S(1)} %copy-done.10, s32[1,4,512]{2,1,0:T(4,128)S(1)} %copy-done.7, s32[1,4,512]{2,1,0:T(4,128)S(1)} %copy-done.8), custom_call_target="tpu_custom_call" | custom-call | flops 67108864 | bytes 1048576 | tf_op jit(solution)/shard_map/pallas_call | solution.py:497
  28.6 9.6 %all-to-all-done.1.arrived = bf16[32,32,128]{2,1,0:T(8,128)(2,1)S(1)} async-done(((bf16[32,32,128]{2,1,0:T(8,128)(2,1)}), bf16[32,32,128]{2,1,0:T(8,128)(2,1)S(1)}, u32[]{:S(2)}, u32[]{:S(2)}) %all-to-all-start.1) | async-done | bytes 262176 | tf_op jit(solution)/shard_map/all_to_all | solution.py:509
  38.2 0.0 copy-done.5
  38.2 1.1 %shard_map.136 = (f32[2,1,4,512]{3,2,1,0:T(4,128)}, bf16[32,32,128]{2,1,0:T(8,128)(2,1)S(1)}) custom-call(s32[1,4]{1,0:T(1,128)S(1)} %copy-done.6, s32[1,128]{1,0:T(1,128)S(1)} %get-tuple-element.10.place, bf16[32,32,128]{2,1,0:T(8,128)(2,1)S(1)} %all-to-all-done.1.arrived, f32[2,1,4,512]{3,2,1,0:T(4,128)S(1)} %copy-done.5, ...), custom_call_target="tpu_custom_call" | custom-call | flops 268435456 | bytes 1048576 | tf_op jit(solution)/shard_map/pallas_call | solution.py:497
  39.4 12.7 %all_to_all.15.refs_1_ = bf16[32,32,128]{2,1,0:T(8,128)(2,1)S(1)} all-to-all(bf16[32,32,128]{2,1,0:T(8,128)(2,1)S(1)} %get-tuple-element.17), channel_id=1, replica_groups=mesh['role'=4,'grp'=2,'rep'=4] {'role','grp','rep'}, dimensions={0} | all-to-all | bytes 524288 | tf_op jit(solution)/shard_map/all_to_all | solution.py:509
  52.1 1.1 %shard_map.137 = bf16[2,8,16,128]{3,2,1,0:T(8,128)(2,1)} custom-call(s32[32,1,128]{2,1,0:T(1,128)S(1)} %all-to-all-done.refs_0_, bf16[32,32,128]{2,1,0:T(8,128)(2,1)S(1)} %all_to_all.15.refs_1_), custom_call_target="tpu_custom_call" | custom-call | flops 67108864 | bytes 1048576 | tf_op jit(solution)/shard_map/pallas_call | solution.py:497
  (4 shorter events, 0.0 us)
Async XLA Ops:
  0.6 0.9 %copy-start = (f32[2,128,128]{2,1,0:T(8,128)S(1)}, f32[2,128,128]{2,1,0:T(8,128)}, u32[]{:S(2)}) copy-start(f32[2,128,128]{2,1,0:T(8,128)} %constant.9.clone.refs_3_) | copy-start | bytes 393220
  1.5 0.9 %copy-start.1 = (f32[2,128,128]{2,1,0:T(8,128)S(1)}, f32[2,128,128]{2,1,0:T(8,128)}, u32[]{:S(2)}) copy-start(f32[2,128,128]{2,1,0:T(8,128)} %constant.8.clone.refs_2_) | copy-start | bytes 393220
  2.4 0.7 %copy-start.4 = (f32[1,4096]{1,0:T(1,128)S(1)}, f32[1,4096]{1,0:T(1,128)}, u32[]{:S(2)}) copy-start(f32[1,4096]{1,0:T(1,128)} %refs_1_.1) | copy-start | bytes 49156
  3.2 5.9 %copy-start.9 = (s32[1,4]{1,0:T(1,128)S(1)}, s32[1,4]{1,0:T(1,128)}, u32[]{:S(2)}) copy-start(s32[1,4]{1,0:T(1,128)} %positions.1) | copy-start | bytes 52
  8.4 8.3 %copy-start.2 = (f32[2,128,128]{2,1,0:T(8,128)S(1)}, f32[2,128,128]{2,1,0:T(8,128)}, u32[]{:S(2)}) copy-start(f32[2,128,128]{2,1,0:T(8,128)} %constant.11.clone.refs_3_) | copy-start | bytes 393220
  8.4 8.3 %copy-start.3 = (f32[2,128,128]{2,1,0:T(8,128)S(1)}, f32[2,128,128]{2,1,0:T(8,128)}, u32[]{:S(2)}) copy-start(f32[2,128,128]{2,1,0:T(8,128)} %constant.10.clone.refs_2_) | copy-start | bytes 393220
  8.4 19.2 %copy-start.7 = (s32[1,4,512]{2,1,0:T(4,128)S(1)}, s32[1,4,512]{2,1,0:T(4,128)}, u32[]{:S(2)}) copy-start(s32[1,4,512]{2,1,0:T(4,128)} %vis_u.1) | copy-start | bytes 24580
  8.4 19.2 %copy-start.8 = (s32[1,4,512]{2,1,0:T(4,128)S(1)}, s32[1,4,512]{2,1,0:T(4,128)}, u32[]{:S(2)}) copy-start(s32[1,4,512]{2,1,0:T(4,128)} %vis_v.1) | copy-start | bytes 24580
  8.4 19.2 %copy-start.10 = (f32[8]{0:T(128)S(1)}, f32[8]{0:T(128)}, u32[]{:S(2)}) copy-start(f32[8]{0:T(128)} %taps.1) | copy-start | bytes 100
  8.4 29.8 %copy-start.5 = (f32[2,1,4,512]{3,2,1,0:T(4,128)S(1)}, f32[2,1,4,512]{3,2,1,0:T(4,128)}, u32[]{:S(2)}) copy-start(f32[2,1,4,512]{3,2,1,0:T(4,128)} %observed.1) | copy-start | bytes 49156
  8.5 29.8 %copy-start.6 = (s32[1,4]{1,0:T(1,128)S(1)}, s32[1,4]{1,0:T(1,128)}, u32[]{:S(2)}) copy-start(s32[1,4]{1,0:T(1,128)} %counts.1) | copy-start | bytes 52
  8.5 8.2 %collective-permute-start = (bf16[512,128]{1,0:T(8,128)(2,1)S(1)}, bf16[512,128]{1,0:T(8,128)(2,1)S(1)}, u32[]{:S(2)}, u32[]{:S(2)}) collective-permute-start(bf16[512,128]{1,0:T(8,128)(2,1)S(1)} %get-tuple-element.13), channel_id=1, source_target_pairs={{0,1},{1,0},{2,3},{3,2},{4,5},{5,4},{6,7},{7,6},{8,9},{9,8},{10,11... | collective-permute-start | bytes 393224 | tf_op jit(solution)/shard_map/ppermute | solution.py:551
  9.7 14.1 %all-to-all-start = ((s32[32,1,128]{2,1,0:T(1,128)}), s32[32,1,128]{2,1,0:T(1,128)S(1)}, u32[]{:S(2)}, u32[]{:S(2)}) async-start(s32[32,1,128]{2,1,0:T(1,128)} %get-tuple-element.11), calls=%async_computation | async-start | bytes 32768 | tf_op jit(solution)/shard_map/all_to_all | solution.py:509
  25.1 13.2 %all-to-all-start.1 = ((bf16[32,32,128]{2,1,0:T(8,128)(2,1)}), bf16[32,32,128]{2,1,0:T(8,128)(2,1)S(1)}, u32[]{:S(2)}, u32[]{:S(2)}) async-start(bf16[32,32,128]{2,1,0:T(8,128)(2,1)} %shard_map.134), calls=%async_computation.1 | async-start | bytes 524288 | tf_op jit(solution)/shard_map/all_to_all | solution.py:509

commit v2 on v1

--- a/solution.py
+++ b/solution.py
@@ -406,9 +406,7 @@
         taps_v[:, span] = taps_of(vis_v[0, p : p + 1, :])
 
 
-def degrid_kernel(
-    counts, place, arrived, observed, taps_u, taps_v, residual_far, out, weighted, residual, sem
-):
+def degrid_kernel(counts, place, arrived, observed, taps_u, taps_v, residual, out, weighted):
     length = observed.shape[-1]
     left = lanes_of((PATCH, LANES)) < LANES // 2
     sums = []
@@ -437,8 +435,6 @@
             weighted[2 * PATCH + c * PATCH : 2 * PATCH + (c + 1) * PATCH, span] = (
                 value - high.astype(jnp.float32)
             ).astype(jnp.bfloat16)
-    copy = pltpu.make_async_copy(residual, residual_far, sem)
-    copy.start()
     product = contract(weighted[...], taps_u[...])
     product = product[: 2 * PATCH] + product[2 * PATCH :]
     gridded = product[:, :LANES] + product[:, LANES:]
@@ -451,10 +447,13 @@
         piece = jnp.where(row == owner // 2, halves[owner % 2], 0.0).astype(jnp.bfloat16)
         for first in range(0, out.shape[0], owners):
             out[first + owner] = piece
-    copy.wait()
-
-
-def return_kernel(rep_count, places, arrived, returned, canvas):
+
+
+def return_kernel(
+    rep_count, places, arrived, residual_near, residual, returned, canvas, sem
+):
+    copy = pltpu.make_async_copy(residual_near, residual, sem)
+    copy.start()
     sub_cols = returned.shape[1]
     col_blocks = (C + 2 * EDGE) // PATCH
     for column in range(sub_cols):
@@ -485,6 +484,7 @@
         value = contract(pick, jnp.concatenate([high, low], axis=1)).astype(jnp.bfloat16)
         for c in range(2):
             returned[c, column] = value[c * HALF : (c + 1) * HALF]
+    copy.wait()
 
 
 def call(kernel, out_shape, operands, scratch, flops, scalars=0, first=None, outs=None, limit=24):
@@ -579,25 +579,26 @@
     arrived = near(exchanged(outgoing))
     residual, gridded = call(
         degrid_kernel,
-        (pltpu.HBM(observed.shape, f32), chunk),
+        (pltpu.VMEM(observed.shape, f32), chunk),
         (near(counts), place, arrived, near(observed), near(taps_u), near(taps_v)),
+        [pltpu.VMEM((4 * PATCH, SLOTS * length), bf16)],
+        1 << 28,
+    )
+    spread = near(exchanged(gridded))
+    return call(
+        lambda *refs: return_kernel(rep_count, *refs),
+        (
+            pltpu.HBM(observed.shape, f32),
+            jax.ShapeDtypeStruct((2, sub_cols, HALF, C), bf16),
+        ),
+        (places, spread, near(residual)),
         [
-            pltpu.VMEM((4 * PATCH, SLOTS * length), bf16),
-            pltpu.VMEM(observed.shape, f32),
+            pltpu.VMEM((sub_cols * col_blocks, PATCH, LANES), f32),
             pltpu.SemaphoreType.DMA,
         ],
-        1 << 28,
+        1 << 26,
         outs=(pltpu.HBM, pltpu.VMEM),
     )
-    spread = near(exchanged(gridded))
-    returned = call(
-        lambda *refs: return_kernel(rep_count, *refs),
-        jax.ShapeDtypeStruct((2, sub_cols, HALF, C), bf16),
-        (places, spread),
-        [pltpu.VMEM((sub_cols * col_blocks, PATCH, LANES), f32)],
-        1 << 26,
-    )
-    return (residual, returned)
 
 
 def part(facets, taper, kernel, observed, patch_pos, counts, vis_u, vis_v):

time: 53.6 us -> 53.3 us (level)
  no operation moved by 1% of the time
where the time goes in v2:
time: 53.3 us; the launch traced here: 53 us
  waiting for transfers between devices  16.1 us (30%)
  blocking collectives  12.7 us (24%)
  Pallas kernels  10.7 us (20%)
  starting transfers between devices  10.1 us (19%)
  local copies, waits for them, and re-layouts  2.57 us (5%)
  between operations  0.8 us (2%)
    all_to_all x2, waiting for transfers between devices, exchanged(): lax.all_to_all(value, EVERYONE, split_axis=0, concat_axis=0, tiled=True)  16.1 us
    all_to_all x1, blocking collectives, exchanged(): lax.all_to_all(value, EVERYONE, split_axis=0, concat_axis=0, tiled=True)  12.7 us
    pallas_call x7, Pallas kernels, call(): pl.pallas_call(kernel, out_shape=out_shape, in_specs=[pl.BlockSpec(memory...  10.7 us
    all_to_all x2, starting transfers between devices, exchanged(): lax.all_to_all(value, EVERYONE, split_axis=0, concat_axis=0, tiled=True)  9.54 us
    unnamed x22, local copies, waits for them, and re-layouts  2.57 us
  transfers between devices with their start and end apart: 3, of which 2 were waited for; matrix products, arithmetic and copies ran while one was open for 0% of the time, Pallas kernels for 4%

profile of v2, /device:TPU:0, one launch (start us, length us, event | category | flops | bytes accessed | tf_op | source)
XLA Modules:
  0.0 53.0 jit_solution(9713159680281621156)
XLA Ops:
  0.6 0.0 copy-start
  0.6 0.9 %copy-done = f32[2,128,128]{2,1,0:T(8,128)S(1)} copy-done((f32[2,128,128]{2,1,0:T(8,128)S(1)}, f32[2,128,128]{2,1,0:T(8,128)}, u32[]{:S(2)}) %copy-start) | copy-done | bytes 131096
  1.5 0.9 %copy-done.1 = f32[2,128,128]{2,1,0:T(8,128)S(1)} copy-done((f32[2,128,128]{2,1,0:T(8,128)S(1)}, f32[2,128,128]{2,1,0:T(8,128)}, u32[]{:S(2)}) %copy-start.1) | copy-done | bytes 131096
  2.4 0.7 %copy-done.4 = f32[1,4096]{1,0:T(1,128)S(1)} copy-done((f32[1,4096]{1,0:T(1,128)S(1)}, f32[1,4096]{1,0:T(1,128)}, u32[]{:S(2)}) %copy-start.4) | copy-done | bytes 16408
  3.2 5.2 %shard_map.132 = (bf16[512,128]{1,0:T(8,128)(2,1)S(1)}, bf16[512,128]{1,0:T(8,128)(2,1)S(1)}) custom-call(bf16[1,2,512,4096]{3,2,1,0:T(8,128)(2,1)} %refs_0_.1, f32[1,4096]{1,0:T(1,128)S(1)} %copy-done.4, f32[2,128,128]{2,1,0:T(8,128)S(1)} %copy-done.1, f32[2,128,128]{2,1,0:T(8,128)S(1)} %copy-done), custom_call_target="tpu_custom_call" | custom-call | flops 2147483648 | bytes 1048576 | tf_op jit(solution)/shard_map/pallas_call | solution.py:497
  8.4 0.0 copy-start.2
  8.4 0.0 copy-start.3
  8.4 0.0 copy-start.7
  8.4 0.0 copy-start.8
  8.4 0.0 copy-start.10
  8.4 0.0 copy-start.5
  8.5 0.0 copy-start.6
  8.5 0.6 %collective-permute-start = (bf16[512,128]{1,0:T(8,128)(2,1)S(1)}, bf16[512,128]{1,0:T(8,128)(2,1)S(1)}, u32[]{:S(2)}, u32[]{:S(2)}) collective-permute-start(bf16[512,128]{1,0:T(8,128)(2,1)S(1)} %get-tuple-element.13), channel_id=1, source_target_pairs={{0,1},{1,0},{2,3},{3,2},{4,5},{5,4},{6,7},{7,6},{8,9},{9,8},{10,11... | collective-permute-start | bytes 393224 | tf_op jit(solution)/shard_map/ppermute | solution.py:551
  9.0 0.0 copy-done.9
  9.0 0.7 %shard_map.131 = (s32[1,128]{1,0:T(1,128)S(1)}, s32[32,1,128]{2,1,0:T(1,128)}) custom-call(s32[1,4]{1,0:T(1,128)S(1)} %copy-done.9), custom_call_target="tpu_custom_call" | custom-call | flops 8589934592 | bytes 1048576 | tf_op jit(solution)/shard_map/pallas_call | solution.py:497
  9.7 7.0 %all-to-all-start = ((s32[32,1,128]{2,1,0:T(1,128)}), s32[32,1,128]{2,1,0:T(1,128)S(1)}, u32[]{:S(2)}, u32[]{:S(2)}) async-start(s32[32,1,128]{2,1,0:T(1,128)} %get-tuple-element.10), calls=%async_computation | async-start | bytes 32768 | tf_op jit(solution)/shard_map/all_to_all | solution.py:509
  16.7 0.0 collective-permute-done.refs_1_
  16.7 0.0 copy-done.2
  16.7 0.0 copy-done.3
  16.7 0.6 %shard_map.133.refs_1_ = f32[1088,128]{1,0:T(8,128)S(1)} custom-call(bf16[512,128]{1,0:T(8,128)(2,1)S(1)} %get-tuple-element.12.refs_0_, bf16[512,128]{1,0:T(8,128)(2,1)S(1)} %collective-permute-done.refs_1_, f32[2,128,128]{2,1,0:T(8,128)S(1)} %copy-done.3, f32[2,128,128]{2,1,0:T(8,128)S(1)} %copy-done.2), custom_call_target="tpu_custom_call" | custom-call | flops 1048576 | bytes 1048576 | tf_op jit(solution)/shard_map/pallas_call | solution.py:497
  17.3 6.5 %all-to-all-done.refs_0_ = s32[32,1,128]{2,1,0:T(1,128)S(1)} async-done(((s32[32,1,128]{2,1,0:T(1,128)}), s32[32,1,128]{2,1,0:T(1,128)S(1)}, u32[]{:S(2)}, u32[]{:S(2)}) %all-to-all-start) | async-done | bytes 16416 | tf_op jit(solution)/shard_map/all_to_all | solution.py:509
  23.8 1.3 %shard_map.134 = bf16[32,32,128]{2,1,0:T(8,128)(2,1)} custom-call(s32[32,1,128]{2,1,0:T(1,128)S(1)} %all-to-all-done.refs_0_, f32[1088,128]{1,0:T(8,128)S(1)} %shard_map.133.refs_1_), custom_call_target="tpu_custom_call" | custom-call | flops 268435456 | bytes 1048576 | tf_op jit(solution)/shard_map/pallas_call | solution.py:497
  25.1 2.6 %all-to-all-start.1 = ((bf16[32,32,128]{2,1,0:T(8,128)(2,1)}), bf16[32,32,128]{2,1,0:T(8,128)(2,1)S(1)}, u32[]{:S(2)}, u32[]{:S(2)}) async-start(bf16[32,32,128]{2,1,0:T(8,128)(2,1)} %shard_map.134), calls=%async_computation.1 | async-start | bytes 524288 | tf_op jit(solution)/shard_map/all_to_all | solution.py:509
  27.7 0.0 copy-done.7
  27.7 0.0 copy-done.8
  27.7 0.0 copy-done.10
  27.7 0.9 %shard_map.135 = (bf16[256,2048]{1,0:T(8,128)(2,1)S(1)}, f32[32,2048]{1,0:T(8,128)S(1)}) custom-call(f32[8]{0:T(128)S(1)} %copy-done.10, s32[1,4,512]{2,1,0:T(4,128)S(1)} %copy-done.7, s32[1,4,512]{2,1,0:T(4,128)S(1)} %copy-done.8), custom_call_target="tpu_custom_call" | custom-call | flops 67108864 | bytes 1048576 | tf_op jit(solution)/shard_map/pallas_call | solution.py:497
  28.6 9.6 %all-to-all-done.1.arrived = bf16[32,32,128]{2,1,0:T(8,128)(2,1)S(1)} async-done(((bf16[32,32,128]{2,1,0:T(8,128)(2,1)}), bf16[32,32,128]{2,1,0:T(8,128)(2,1)S(1)}, u32[]{:S(2)}, u32[]{:S(2)}) %all-to-all-start.1) | async-done | bytes 262176 | tf_op jit(solution)/shard_map/all_to_all | solution.py:509
  38.2 0.0 copy-done.5
  38.2 0.8 %shard_map.136 = (f32[2,1,4,512]{3,2,1,0:T(4,128)S(1)}, bf16[32,32,128]{2,1,0:T(8,128)(2,1)S(1)}) custom-call(s32[1,4]{1,0:T(1,128)S(1)} %copy-done.6, s32[1,128]{1,0:T(1,128)S(1)} %get-tuple-element.11.place, bf16[32,32,128]{2,1,0:T(8,128)(2,1)S(1)} %all-to-all-done.1.arrived, f32[2,1,4,512]{3,2,1,0:T(4,128)S(1)} %copy-done.5, ...), custom_call_target="tpu_custom_call" | custom-call | flops 268435456 | bytes 1048576 | tf_op jit(solution)/shard_map/pallas_call | solution.py:497
  39.0 12.7 %all_to_all.15.refs_1_ = bf16[32,32,128]{2,1,0:T(8,128)(2,1)S(1)} all-to-all(bf16[32,32,128]{2,1,0:T(8,128)(2,1)S(1)} %get-tuple-element.16), channel_id=1, replica_groups=mesh['role'=4,'grp'=2,'rep'=4] {'role','grp','rep'}, dimensions={0} | all-to-all | bytes 524288 | tf_op jit(solution)/shard_map/all_to_all | solution.py:509
  51.7 1.3 %shard_map.137 = (f32[2,1,4,512]{3,2,1,0:T(4,128)}, bf16[2,8,16,128]{3,2,1,0:T(8,128)(2,1)}) custom-call(s32[32,1,128]{2,1,0:T(1,128)S(1)} %all-to-all-done.refs_0_, bf16[32,32,128]{2,1,0:T(8,128)(2,1)S(1)} %all_to_all.15.refs_1_, f32[2,1,4,512]{3,2,1,0:T(4,128)S(1)} %get-tuple-element.17.refs_2_), custom_call_target="tpu_custom_call" | custom-call | flops 67108864 | bytes 1048576 | tf_op jit(solution)/shard_map/pallas_call | solution.py:497
  (4 shorter events, 0.0 us)
Async XLA Ops:
  0.6 0.9 %copy-start = (f32[2,128,128]{2,1,0:T(8,128)S(1)}, f32[2,128,128]{2,1,0:T(8,128)}, u32[]{:S(2)}) copy-start(f32[2,128,128]{2,1,0:T(8,128)} %constant.9.clone.refs_3_) | copy-start | bytes 393220
  1.5 0.9 %copy-start.1 = (f32[2,128,128]{2,1,0:T(8,128)S(1)}, f32[2,128,128]{2,1,0:T(8,128)}, u32[]{:S(2)}) copy-start(f32[2,128,128]{2,1,0:T(8,128)} %constant.8.clone.refs_2_) | copy-start | bytes 393220
  2.4 0.7 %copy-start.4 = (f32[1,4096]{1,0:T(1,128)S(1)}, f32[1,4096]{1,0:T(1,128)}, u32[]{:S(2)}) copy-start(f32[1,4096]{1,0:T(1,128)} %refs_1_.1) | copy-start | bytes 49156
  3.2 5.9 %copy-start.9 = (s32[1,4]{1,0:T(1,128)S(1)}, s32[1,4]{1,0:T(1,128)}, u32[]{:S(2)}) copy-start(s32[1,4]{1,0:T(1,128)} %positions.1) | copy-start | bytes 52
  8.4 8.3 %copy-start.2 = (f32[2,128,128]{2,1,0:T(8,128)S(1)}, f32[2,128,128]{2,1,0:T(8,128)}, u32[]{:S(2)}) copy-start(f32[2,128,128]{2,1,0:T(8,128)} %constant.11.clone.refs_3_) | copy-start | bytes 393220
  8.4 8.3 %copy-start.3 = (f32[2,128,128]{2,1,0:T(8,128)S(1)}, f32[2,128,128]{2,1,0:T(8,128)}, u32[]{:S(2)}) copy-start(f32[2,128,128]{2,1,0:T(8,128)} %constant.10.clone.refs_2_) | copy-start | bytes 393220
  8.4 19.2 %copy-start.7 = (s32[1,4,512]{2,1,0:T(4,128)S(1)}, s32[1,4,512]{2,1,0:T(4,128)}, u32[]{:S(2)}) copy-start(s32[1,4,512]{2,1,0:T(4,128)} %vis_u.1) | copy-start | bytes 24580
  8.4 19.2 %copy-start.8 = (s32[1,4,512]{2,1,0:T(4,128)S(1)}, s32[1,4,512]{2,1,0:T(4,128)}, u32[]{:S(2)}) copy-start(s32[1,4,512]{2,1,0:T(4,128)} %vis_v.1) | copy-start | bytes 24580
  8.4 19.2 %copy-start.10 = (f32[8]{0:T(128)S(1)}, f32[8]{0:T(128)}, u32[]{:S(2)}) copy-start(f32[8]{0:T(128)} %taps.1) | copy-start | bytes 100
  8.4 29.8 %copy-start.5 = (f32[2,1,4,512]{3,2,1,0:T(4,128)S(1)}, f32[2,1,4,512]{3,2,1,0:T(4,128)}, u32[]{:S(2)}) copy-start(f32[2,1,4,512]{3,2,1,0:T(4,128)} %observed.1) | copy-start | bytes 49156
  8.5 29.8 %copy-start.6 = (s32[1,4]{1,0:T(1,128)S(1)}, s32[1,4]{1,0:T(1,128)}, u32[]{:S(2)}) copy-start(s32[1,4]{1,0:T(1,128)} %counts.1) | copy-start | bytes 52
  8.5 8.2 %collective-permute-start = (bf16[512,128]{1,0:T(8,128)(2,1)S(1)}, bf16[512,128]{1,0:T(8,128)(2,1)S(1)}, u32[]{:S(2)}, u32[]{:S(2)}) collective-permute-start(bf16[512,128]{1,0:T(8,128)(2,1)S(1)} %get-tuple-element.13), channel_id=1, source_target_pairs={{0,1},{1,0},{2,3},{3,2},{4,5},{5,4},{6,7},{7,6},{8,9},{9,8},{10,11... | collective-permute-start | bytes 393224 | tf_op jit(solution)/shard_map/ppermute | solution.py:551
  9.7 14.1 %all-to-all-start = ((s32[32,1,128]{2,1,0:T(1,128)}), s32[32,1,128]{2,1,0:T(1,128)S(1)}, u32[]{:S(2)}, u32[]{:S(2)}) async-start(s32[32,1,128]{2,1,0:T(1,128)} %get-tuple-element.10), calls=%async_computation | async-start | bytes 32768 | tf_op jit(solution)/shard_map/all_to_all | solution.py:509
  25.1 13.2 %all-to-all-start.1 = ((bf16[32,32,128]{2,1,0:T(8,128)(2,1)}), bf16[32,32,128]{2,1,0:T(8,128)(2,1)S(1)}, u32[]{:S(2)}, u32[]{:S(2)}) async-start(bf16[32,32,128]{2,1,0:T(8,128)(2,1)} %shard_map.134), calls=%async_computation.1 | async-start | bytes 524288 | tf_op jit(solution)/shard_map/all_to_all | solution.py:509

commit v3 on v2

--- a/solution.py
+++ b/solution.py
@@ -450,10 +450,10 @@
 
 
 def return_kernel(
-    rep_count, places, arrived, residual_near, residual, returned, canvas, sem
+    rep_count, places, arrived, residual_near, residual, returned_far, canvas, returned, sem, sems
 ):
-    copy = pltpu.make_async_copy(residual_near, residual, sem)
-    copy.start()
+    copies = [pltpu.make_async_copy(residual_near, residual, sem)]
+    copies[0].start()
     sub_cols = returned.shape[1]
     col_blocks = (C + 2 * EDGE) // PATCH
     for column in range(sub_cols):
@@ -484,7 +484,16 @@
         value = contract(pick, jnp.concatenate([high, low], axis=1)).astype(jnp.bfloat16)
         for c in range(2):
             returned[c, column] = value[c * HALF : (c + 1) * HALF]
-    copy.wait()
+        if column % 4 == 3:
+            columns = slice(column - 3, column + 1)
+            copies.append(
+                pltpu.make_async_copy(
+                    returned.at[:, columns], returned_far.at[:, columns], sems.at[column // 4]
+                )
+            )
+            copies[-1].start()
+    for copy in copies:
+        copy.wait()
 
 
 def call(kernel, out_shape, operands, scratch, flops, scalars=0, first=None, outs=None, limit=24):
@@ -589,15 +598,17 @@
         lambda *refs: return_kernel(rep_count, *refs),
         (
             pltpu.HBM(observed.shape, f32),
-            jax.ShapeDtypeStruct((2, sub_cols, HALF, C), bf16),
+            pltpu.HBM((2, sub_cols, HALF, C), bf16),
         ),
         (places, spread, near(residual)),
         [
             pltpu.VMEM((sub_cols * col_blocks, PATCH, LANES), f32),
+            pltpu.VMEM((2, sub_cols, HALF, C), bf16),
             pltpu.SemaphoreType.DMA,
+            pltpu.SemaphoreType.DMA((sub_cols // 4,)),
         ],
         1 << 26,
-        outs=(pltpu.HBM, pltpu.VMEM),
+        outs=(pltpu.HBM, pltpu.HBM),
     )
 
 

time: 53.3 us -> 53.2 us (level)
  no operation moved by 1% of the time
where the time goes in v3:
time: 53.2 us; the launch traced here: 52.8 us
  waiting for transfers between devices  16.1 us (30%)
  blocking collectives  12.7 us (24%)
  Pallas kernels  10.6 us (20%)
  starting transfers between devices  10.1 us (19%)
  local copies, waits for them, and re-layouts  2.57 us (5%)
  between operations  0.8 us (2%)
    all_to_all x2, waiting for transfers between devices, exchanged(): lax.all_to_all(value, EVERYONE, split_axis=0, concat_axis=0, tiled=True)  16.1 us
    all_to_all x1, blocking collectives, exchanged(): lax.all_to_all(value, EVERYONE, split_axis=0, concat_axis=0, tiled=True)  12.7 us
    pallas_call x7, Pallas kernels, call(): pl.pallas_call(kernel, out_shape=out_shape, in_specs=[pl.BlockSpec(memory...  10.6 us
    all_to_all x2, starting transfers between devices, exchanged(): lax.all_to_all(value, EVERYONE, split_axis=0, concat_axis=0, tiled=True)  9.54 us
    unnamed x22, local copies, waits for them, and re-layouts  2.57 us
  transfers between devices with their start and end apart: 3, of which 2 were waited for; matrix products, arithmetic and copies ran while one was open for 0% of the time, Pallas kernels for 4%

profile of v3, /device:TPU:0, one launch (start us, length us, event | category | flops | bytes accessed | tf_op | source)
XLA Modules:
  0.0 52.8 jit_solution(15697845902932854774)
XLA Ops:
  0.6 0.0 copy-start
  0.6 0.9 %copy-done = f32[2,128,128]{2,1,0:T(8,128)S(1)} copy-done((f32[2,128,128]{2,1,0:T(8,128)S(1)}, f32[2,128,128]{2,1,0:T(8,128)}, u32[]{:S(2)}) %copy-start) | copy-done | bytes 131096
  1.5 0.9 %copy-done.1 = f32[2,128,128]{2,1,0:T(8,128)S(1)} copy-done((f32[2,128,128]{2,1,0:T(8,128)S(1)}, f32[2,128,128]{2,1,0:T(8,128)}, u32[]{:S(2)}) %copy-start.1) | copy-done | bytes 131096
  2.4 0.7 %copy-done.4 = f32[1,4096]{1,0:T(1,128)S(1)} copy-done((f32[1,4096]{1,0:T(1,128)S(1)}, f32[1,4096]{1,0:T(1,128)}, u32[]{:S(2)}) %copy-start.4) | copy-done | bytes 16408
  3.2 5.2 %shard_map.132 = (bf16[512,128]{1,0:T(8,128)(2,1)S(1)}, bf16[512,128]{1,0:T(8,128)(2,1)S(1)}) custom-call(bf16[1,2,512,4096]{3,2,1,0:T(8,128)(2,1)} %refs_0_.1, f32[1,4096]{1,0:T(1,128)S(1)} %copy-done.4, f32[2,128,128]{2,1,0:T(8,128)S(1)} %copy-done.1, f32[2,128,128]{2,1,0:T(8,128)S(1)} %copy-done), custom_call_target="tpu_custom_call" | custom-call | flops 2147483648 | bytes 1048576 | tf_op jit(solution)/shard_map/pallas_call | solution.py:506
  8.4 0.0 copy-start.2
  8.4 0.0 copy-start.3
  8.4 0.0 copy-start.7
  8.4 0.0 copy-start.8
  8.4 0.0 copy-start.10
  8.4 0.0 copy-start.5
  8.5 0.0 copy-start.6
  8.5 0.6 %collective-permute-start = (bf16[512,128]{1,0:T(8,128)(2,1)S(1)}, bf16[512,128]{1,0:T(8,128)(2,1)S(1)}, u32[]{:S(2)}, u32[]{:S(2)}) collective-permute-start(bf16[512,128]{1,0:T(8,128)(2,1)S(1)} %get-tuple-element.13), channel_id=1, source_target_pairs={{0,1},{1,0},{2,3},{3,2},{4,5},{5,4},{6,7},{7,6},{8,9},{9,8},{10,11... | collective-permute-start | bytes 393224 | tf_op jit(solution)/shard_map/ppermute | solution.py:560
  9.0 0.0 copy-done.9
  9.0 0.7 %shard_map.131 = (s32[1,128]{1,0:T(1,128)S(1)}, s32[32,1,128]{2,1,0:T(1,128)}) custom-call(s32[1,4]{1,0:T(1,128)S(1)} %copy-done.9), custom_call_target="tpu_custom_call" | custom-call | flops 8589934592 | bytes 1048576 | tf_op jit(solution)/shard_map/pallas_call | solution.py:506
  9.7 7.0 %all-to-all-start = ((s32[32,1,128]{2,1,0:T(1,128)}), s32[32,1,128]{2,1,0:T(1,128)S(1)}, u32[]{:S(2)}, u32[]{:S(2)}) async-start(s32[32,1,128]{2,1,0:T(1,128)} %get-tuple-element.10), calls=%async_computation | async-start | bytes 32768 | tf_op jit(solution)/shard_map/all_to_all | solution.py:518
  16.7 0.0 collective-permute-done.refs_1_
  16.7 0.0 copy-done.2
  16.7 0.0 copy-done.3
  16.7 0.6 %shard_map.133.refs_1_ = f32[1088,128]{1,0:T(8,128)S(1)} custom-call(bf16[512,128]{1,0:T(8,128)(2,1)S(1)} %get-tuple-element.12.refs_0_, bf16[512,128]{1,0:T(8,128)(2,1)S(1)} %collective-permute-done.refs_1_, f32[2,128,128]{2,1,0:T(8,128)S(1)} %copy-done.3, f32[2,128,128]{2,1,0:T(8,128)S(1)} %copy-done.2), custom_call_target="tpu_custom_call" | custom-call | flops 1048576 | bytes 1048576 | tf_op jit(solution)/shard_map/pallas_call | solution.py:506
  17.3 6.5 %all-to-all-done.refs_0_ = s32[32,1,128]{2,1,0:T(1,128)S(1)} async-done(((s32[32,1,128]{2,1,0:T(1,128)}), s32[32,1,128]{2,1,0:T(1,128)S(1)}, u32[]{:S(2)}, u32[]{:S(2)}) %all-to-all-start) | async-done | bytes 16416 | tf_op jit(solution)/shard_map/all_to_all | solution.py:518
  23.8 1.3 %shard_map.134 = bf16[32,32,128]{2,1,0:T(8,128)(2,1)} custom-call(s32[32,1,128]{2,1,0:T(1,128)S(1)} %all-to-all-done.refs_0_, f32[1088,128]{1,0:T(8,128)S(1)} %shard_map.133.refs_1_), custom_call_target="tpu_custom_call" | custom-call | flops 268435456 | bytes 1048576 | tf_op jit(solution)/shard_map/pallas_call | solution.py:506
  25.1 2.6 %all-to-all-start.1 = ((bf16[32,32,128]{2,1,0:T(8,128)(2,1)}), bf16[32,32,128]{2,1,0:T(8,128)(2,1)S(1)}, u32[]{:S(2)}, u32[]{:S(2)}) async-start(bf16[32,32,128]{2,1,0:T(8,128)(2,1)} %shard_map.134), calls=%async_computation.1 | async-start | bytes 524288 | tf_op jit(solution)/shard_map/all_to_all | solution.py:518
  27.7 0.0 copy-done.7
  27.7 0.0 copy-done.8
  27.7 0.0 copy-done.10
  27.7 0.9 %shard_map.135 = (bf16[256,2048]{1,0:T(8,128)(2,1)S(1)}, f32[32,2048]{1,0:T(8,128)S(1)}) custom-call(f32[8]{0:T(128)S(1)} %copy-done.10, s32[1,4,512]{2,1,0:T(4,128)S(1)} %copy-done.7, s32[1,4,512]{2,1,0:T(4,128)S(1)} %copy-done.8), custom_call_target="tpu_custom_call" | custom-call | flops 67108864 | bytes 1048576 | tf_op jit(solution)/shard_map/pallas_call | solution.py:506
  28.6 9.6 %all-to-all-done.1.arrived = bf16[32,32,128]{2,1,0:T(8,128)(2,1)S(1)} async-done(((bf16[32,32,128]{2,1,0:T(8,128)(2,1)}), bf16[32,32,128]{2,1,0:T(8,128)(2,1)S(1)}, u32[]{:S(2)}, u32[]{:S(2)}) %all-to-all-start.1) | async-done | bytes 262176 | tf_op jit(solution)/shard_map/all_to_all | solution.py:518
  38.2 0.0 copy-done.5
  38.2 0.8 %shard_map.136 = (f32[2,1,4,512]{3,2,1,0:T(4,128)S(1)}, bf16[32,32,128]{2,1,0:T(8,128)(2,1)S(1)}) custom-call(s32[1,4]{1,0:T(1,128)S(1)} %copy-done.6, s32[1,128]{1,0:T(1,128)S(1)} %get-tuple-element.11.place, bf16[32,32,128]{2,1,0:T(8,128)(2,1)S(1)} %all-to-all-done.1.arrived, f32[2,1,4,512]{3,2,1,0:T(4,128)S(1)} %copy-done.5, ...), custom_call_target="tpu_custom_call" | custom-call | flops 268435456 | bytes 1048576 | tf_op jit(solution)/shard_map/pallas_call | solution.py:506
  39.0 12.7 %all_to_all.15.refs_1_ = bf16[32,32,128]{2,1,0:T(8,128)(2,1)S(1)} all-to-all(bf16[32,32,128]{2,1,0:T(8,128)(2,1)S(1)} %get-tuple-element.16), channel_id=1, replica_groups=mesh['role'=4,'grp'=2,'rep'=4] {'role','grp','rep'}, dimensions={0} | all-to-all | bytes 524288 | tf_op jit(solution)/shard_map/all_to_all | solution.py:518
  51.7 1.1 %shard_map.137 = (f32[2,1,4,512]{3,2,1,0:T(4,128)}, bf16[2,8,16,128]{3,2,1,0:T(8,128)(2,1)}) custom-call(s32[32,1,128]{2,1,0:T(1,128)S(1)} %all-to-all-done.refs_0_, bf16[32,32,128]{2,1,0:T(8,128)(2,1)S(1)} %all_to_all.15.refs_1_, f32[2,1,4,512]{3,2,1,0:T(4,128)S(1)} %get-tuple-element.17.refs_2_), custom_call_target="tpu_custom_call" | custom-call | flops 67108864 | bytes 1048576 | tf_op jit(solution)/shard_map/pallas_call | solution.py:506
  (4 shorter events, 0.0 us)
Async XLA Ops:
  0.6 0.9 %copy-start = (f32[2,128,128]{2,1,0:T(8,128)S(1)}, f32[2,128,128]{2,1,0:T(8,128)}, u32[]{:S(2)}) copy-start(f32[2,128,128]{2,1,0:T(8,128)} %constant.9.clone.refs_3_) | copy-start | bytes 393220
  1.5 0.9 %copy-start.1 = (f32[2,128,128]{2,1,0:T(8,128)S(1)}, f32[2,128,128]{2,1,0:T(8,128)}, u32[]{:S(2)}) copy-start(f32[2,128,128]{2,1,0:T(8,128)} %constant.8.clone.refs_2_) | copy-start | bytes 393220
  2.4 0.7 %copy-start.4 = (f32[1,4096]{1,0:T(1,128)S(1)}, f32[1,4096]{1,0:T(1,128)}, u32[]{:S(2)}) copy-start(f32[1,4096]{1,0:T(1,128)} %refs_1_.1) | copy-start | bytes 49156
  3.2 5.9 %copy-start.9 = (s32[1,4]{1,0:T(1,128)S(1)}, s32[1,4]{1,0:T(1,128)}, u32[]{:S(2)}) copy-start(s32[1,4]{1,0:T(1,128)} %positions.1) | copy-start | bytes 52
  8.4 8.3 %copy-start.2 = (f32[2,128,128]{2,1,0:T(8,128)S(1)}, f32[2,128,128]{2,1,0:T(8,128)}, u32[]{:S(2)}) copy-start(f32[2,128,128]{2,1,0:T(8,128)} %constant.11.clone.refs_3_) | copy-start | bytes 393220
  8.4 8.3 %copy-start.3 = (f32[2,128,128]{2,1,0:T(8,128)S(1)}, f32[2,128,128]{2,1,0:T(8,128)}, u32[]{:S(2)}) copy-start(f32[2,128,128]{2,1,0:T(8,128)} %constant.10.clone.refs_2_) | copy-start | bytes 393220
  8.4 19.2 %copy-start.7 = (s32[1,4,512]{2,1,0:T(4,128)S(1)}, s32[1,4,512]{2,1,0:T(4,128)}, u32[]{:S(2)}) copy-start(s32[1,4,512]{2,1,0:T(4,128)} %vis_u.1) | copy-start | bytes 24580
  8.4 19.2 %copy-start.8 = (s32[1,4,512]{2,1,0:T(4,128)S(1)}, s32[1,4,512]{2,1,0:T(4,128)}, u32[]{:S(2)}) copy-start(s32[1,4,512]{2,1,0:T(4,128)} %vis_v.1) | copy-start | bytes 24580
  8.4 19.2 %copy-start.10 = (f32[8]{0:T(128)S(1)}, f32[8]{0:T(128)}, u32[]{:S(2)}) copy-start(f32[8]{0:T(128)} %taps.1) | copy-start | bytes 100
  8.4 29.8 %copy-start.5 = (f32[2,1,4,512]{3,2,1,0:T(4,128)S(1)}, f32[2,1,4,512]{3,2,1,0:T(4,128)}, u32[]{:S(2)}) copy-start(f32[2,1,4,512]{3,2,1,0:T(4,128)} %observed.1) | copy-start | bytes 49156
  8.5 29.8 %copy-start.6 = (s32[1,4]{1,0:T(1,128)S(1)}, s32[1,4]{1,0:T(1,128)}, u32[]{:S(2)}) copy-start(s32[1,4]{1,0:T(1,128)} %counts.1) | copy-start | bytes 52
  8.5 8.2 %collective-permute-start = (bf16[512,128]{1,0:T(8,128)(2,1)S(1)}, bf16[512,128]{1,0:T(8,128)(2,1)S(1)}, u32[]{:S(2)}, u32[]{:S(2)}) collective-permute-start(bf16[512,128]{1,0:T(8,128)(2,1)S(1)} %get-tuple-element.13), channel_id=1, source_target_pairs={{0,1},{1,0},{2,3},{3,2},{4,5},{5,4},{6,7},{7,6},{8,9},{9,8},{10,11... | collective-permute-start | bytes 393224 | tf_op jit(solution)/shard_map/ppermute | solution.py:560
  9.7 14.1 %all-to-all-start = ((s32[32,1,128]{2,1,0:T(1,128)}), s32[32,1,128]{2,1,0:T(1,128)S(1)}, u32[]{:S(2)}, u32[]{:S(2)}) async-start(s32[32,1,128]{2,1,0:T(1,128)} %get-tuple-element.10), calls=%async_computation | async-start | bytes 32768 | tf_op jit(solution)/shard_map/all_to_all | solution.py:518
  25.1 13.2 %all-to-all-start.1 = ((bf16[32,32,128]{2,1,0:T(8,128)(2,1)}), bf16[32,32,128]{2,1,0:T(8,128)(2,1)S(1)}, u32[]{:S(2)}, u32[]{:S(2)}) async-start(bf16[32,32,128]{2,1,0:T(8,128)(2,1)} %shard_map.134), calls=%async_computation.1 | async-start | bytes 524288 | tf_op jit(solution)/shard_map/all_to_all | solution.py:518

commit v4 on v3

--- a/solution.py
+++ b/solution.py
@@ -484,11 +484,11 @@
         value = contract(pick, jnp.concatenate([high, low], axis=1)).astype(jnp.bfloat16)
         for c in range(2):
             returned[c, column] = value[c * HALF : (c + 1) * HALF]
-        if column % 4 == 3:
-            columns = slice(column - 3, column + 1)
+        if column % 2 == 1:
+            columns = slice(column - 1, column + 1)
             copies.append(
                 pltpu.make_async_copy(
-                    returned.at[:, columns], returned_far.at[:, columns], sems.at[column // 4]
+                    returned.at[:, columns], returned_far.at[:, columns], sems.at[column // 2]
                 )
             )
             copies[-1].start()
@@ -605,7 +605,7 @@
             pltpu.VMEM((sub_cols * col_blocks, PATCH, LANES), f32),
             pltpu.VMEM((2, sub_cols, HALF, C), bf16),
             pltpu.SemaphoreType.DMA,
-            pltpu.SemaphoreType.DMA((sub_cols // 4,)),
+            pltpu.SemaphoreType.DMA((sub_cols // 2,)),
         ],
         1 << 26,
         outs=(pltpu.HBM, pltpu.HBM),

time: 53.2 us -> 53.2 us (level)
  no operation moved by 1% of the time
where the time goes in v4:
time: 53.2 us; the launch traced here: 52.8 us
  waiting for transfers between devices  16.1 us (30%)
  blocking collectives  12.7 us (24%)
  Pallas kernels  10.6 us (20%)
  starting transfers between devices  10.1 us (19%)
  local copies, waits for them, and re-layouts  2.57 us (5%)
  between operations  0.8 us (2%)
    all_to_all x2, waiting for transfers between devices, exchanged(): lax.all_to_all(value, EVERYONE, split_axis=0, concat_axis=0, tiled=True)  16.1 us
    all_to_all x1, blocking collectives, exchanged(): lax.all_to_all(value, EVERYONE, split_axis=0, concat_axis=0, tiled=True)  12.7 us
    pallas_call x7, Pallas kernels, call(): pl.pallas_call(kernel, out_shape=out_shape, in_specs=[pl.BlockSpec(memory...  10.6 us
    all_to_all x2, starting transfers between devices, exchanged(): lax.all_to_all(value, EVERYONE, split_axis=0, concat_axis=0, tiled=True)  9.54 us
    unnamed x22, local copies, waits for them, and re-layouts  2.57 us
  transfers between devices with their start and end apart: 3, of which 2 were waited for; matrix products, arithmetic and copies ran while one was open for 0% of the time, Pallas kernels for 4%

profile of v4, /device:TPU:0, one launch (start us, length us, event | category | flops | bytes accessed | tf_op | source)
XLA Modules:
  0.0 52.8 jit_solution(1794620282880684126)
XLA Ops:
  0.6 0.0 copy-start
  0.6 0.9 %copy-done = f32[2,128,128]{2,1,0:T(8,128)S(1)} copy-done((f32[2,128,128]{2,1,0:T(8,128)S(1)}, f32[2,128,128]{2,1,0:T(8,128)}, u32[]{:S(2)}) %copy-start) | copy-done | bytes 131096
  1.5 0.9 %copy-done.1 = f32[2,128,128]{2,1,0:T(8,128)S(1)} copy-done((f32[2,128,128]{2,1,0:T(8,128)S(1)}, f32[2,128,128]{2,1,0:T(8,128)}, u32[]{:S(2)}) %copy-start.1) | copy-done | bytes 131096
  2.4 0.7 %copy-done.4 = f32[1,4096]{1,0:T(1,128)S(1)} copy-done((f32[1,4096]{1,0:T(1,128)S(1)}, f32[1,4096]{1,0:T(1,128)}, u32[]{:S(2)}) %copy-start.4) | copy-done | bytes 16408
  3.2 5.2 %shard_map.132 = (bf16[512,128]{1,0:T(8,128)(2,1)S(1)}, bf16[512,128]{1,0:T(8,128)(2,1)S(1)}) custom-call(bf16[1,2,512,4096]{3,2,1,0:T(8,128)(2,1)} %refs_0_.1, f32[1,4096]{1,0:T(1,128)S(1)} %copy-done.4, f32[2,128,128]{2,1,0:T(8,128)S(1)} %copy-done.1, f32[2,128,128]{2,1,0:T(8,128)S(1)} %copy-done), custom_call_target="tpu_custom_call" | custom-call | flops 2147483648 | bytes 1048576 | tf_op jit(solution)/shard_map/pallas_call | solution.py:506
  8.4 0.0 copy-start.2
  8.4 0.0 copy-start.3
  8.4 0.0 copy-start.7
  8.4 0.0 copy-start.8
  8.4 0.0 copy-start.10
  8.4 0.0 copy-start.5
  8.5 0.0 copy-start.6
  8.5 0.6 %collective-permute-start = (bf16[512,128]{1,0:T(8,128)(2,1)S(1)}, bf16[512,128]{1,0:T(8,128)(2,1)S(1)}, u32[]{:S(2)}, u32[]{:S(2)}) collective-permute-start(bf16[512,128]{1,0:T(8,128)(2,1)S(1)} %get-tuple-element.13), channel_id=1, source_target_pairs={{0,1},{1,0},{2,3},{3,2},{4,5},{5,4},{6,7},{7,6},{8,9},{9,8},{10,11... | collective-permute-start | bytes 393224 | tf_op jit(solution)/shard_map/ppermute | solution.py:560
  9.0 0.0 copy-done.9
  9.0 0.7 %shard_map.131 = (s32[1,128]{1,0:T(1,128)S(1)}, s32[32,1,128]{2,1,0:T(1,128)}) custom-call(s32[1,4]{1,0:T(1,128)S(1)} %copy-done.9), custom_call_target="tpu_custom_call" | custom-call | flops 8589934592 | bytes 1048576 | tf_op jit(solution)/shard_map/pallas_call | solution.py:506
  9.7 7.0 %all-to-all-start = ((s32[32,1,128]{2,1,0:T(1,128)}), s32[32,1,128]{2,1,0:T(1,128)S(1)}, u32[]{:S(2)}, u32[]{:S(2)}) async-start(s32[32,1,128]{2,1,0:T(1,128)} %get-tuple-element.10), calls=%async_computation | async-start | bytes 32768 | tf_op jit(solution)/shard_map/all_to_all | solution.py:518
  16.7 0.0 collective-permute-done.refs_1_
  16.7 0.0 copy-done.2
  16.7 0.0 copy-done.3
  16.7 0.6 %shard_map.133.refs_1_ = f32[1088,128]{1,0:T(8,128)S(1)} custom-call(bf16[512,128]{1,0:T(8,128)(2,1)S(1)} %get-tuple-element.12.refs_0_, bf16[512,128]{1,0:T(8,128)(2,1)S(1)} %collective-permute-done.refs_1_, f32[2,128,128]{2,1,0:T(8,128)S(1)} %copy-done.3, f32[2,128,128]{2,1,0:T(8,128)S(1)} %copy-done.2), custom_call_target="tpu_custom_call" | custom-call | flops 1048576 | bytes 1048576 | tf_op jit(solution)/shard_map/pallas_call | solution.py:506
  17.3 6.5 %all-to-all-done.refs_0_ = s32[32,1,128]{2,1,0:T(1,128)S(1)} async-done(((s32[32,1,128]{2,1,0:T(1,128)}), s32[32,1,128]{2,1,0:T(1,128)S(1)}, u32[]{:S(2)}, u32[]{:S(2)}) %all-to-all-start) | async-done | bytes 16416 | tf_op jit(solution)/shard_map/all_to_all | solution.py:518
  23.8 1.3 %shard_map.134 = bf16[32,32,128]{2,1,0:T(8,128)(2,1)} custom-call(s32[32,1,128]{2,1,0:T(1,128)S(1)} %all-to-all-done.refs_0_, f32[1088,128]{1,0:T(8,128)S(1)} %shard_map.133.refs_1_), custom_call_target="tpu_custom_call" | custom-call | flops 268435456 | bytes 1048576 | tf_op jit(solution)/shard_map/pallas_call | solution.py:506
  25.1 2.6 %all-to-all-start.1 = ((bf16[32,32,128]{2,1,0:T(8,128)(2,1)}), bf16[32,32,128]{2,1,0:T(8,128)(2,1)S(1)}, u32[]{:S(2)}, u32[]{:S(2)}) async-start(bf16[32,32,128]{2,1,0:T(8,128)(2,1)} %shard_map.134), calls=%async_computation.1 | async-start | bytes 524288 | tf_op jit(solution)/shard_map/all_to_all | solution.py:518
  27.7 0.0 copy-done.7
  27.7 0.0 copy-done.8
  27.7 0.0 copy-done.10
  27.7 0.9 %shard_map.135 = (bf16[256,2048]{1,0:T(8,128)(2,1)S(1)}, f32[32,2048]{1,0:T(8,128)S(1)}) custom-call(f32[8]{0:T(128)S(1)} %copy-done.10, s32[1,4,512]{2,1,0:T(4,128)S(1)} %copy-done.7, s32[1,4,512]{2,1,0:T(4,128)S(1)} %copy-done.8), custom_call_target="tpu_custom_call" | custom-call | flops 67108864 | bytes 1048576 | tf_op jit(solution)/shard_map/pallas_call | solution.py:506
  28.6 9.6 %all-to-all-done.1.arrived = bf16[32,32,128]{2,1,0:T(8,128)(2,1)S(1)} async-done(((bf16[32,32,128]{2,1,0:T(8,128)(2,1)}), bf16[32,32,128]{2,1,0:T(8,128)(2,1)S(1)}, u32[]{:S(2)}, u32[]{:S(2)}) %all-to-all-start.1) | async-done | bytes 262176 | tf_op jit(solution)/shard_map/all_to_all | solution.py:518
  38.2 0.0 copy-done.5
  38.2 0.8 %shard_map.136 = (f32[2,1,4,512]{3,2,1,0:T(4,128)S(1)}, bf16[32,32,128]{2,1,0:T(8,128)(2,1)S(1)}) custom-call(s32[1,4]{1,0:T(1,128)S(1)} %copy-done.6, s32[1,128]{1,0:T(1,128)S(1)} %get-tuple-element.11.place, bf16[32,32,128]{2,1,0:T(8,128)(2,1)S(1)} %all-to-all-done.1.arrived, f32[2,1,4,512]{3,2,1,0:T(4,128)S(1)} %copy-done.5, ...), custom_call_target="tpu_custom_call" | custom-call | flops 268435456 | bytes 1048576 | tf_op jit(solution)/shard_map/pallas_call | solution.py:506
  39.0 12.7 %all_to_all.15.refs_1_ = bf16[32,32,128]{2,1,0:T(8,128)(2,1)S(1)} all-to-all(bf16[32,32,128]{2,1,0:T(8,128)(2,1)S(1)} %get-tuple-element.16), channel_id=1, replica_groups=mesh['role'=4,'grp'=2,'rep'=4] {'role','grp','rep'}, dimensions={0} | all-to-all | bytes 524288 | tf_op jit(solution)/shard_map/all_to_all | solution.py:518
  51.7 1.1 %shard_map.137 = (f32[2,1,4,512]{3,2,1,0:T(4,128)}, bf16[2,8,16,128]{3,2,1,0:T(8,128)(2,1)}) custom-call(s32[32,1,128]{2,1,0:T(1,128)S(1)} %all-to-all-done.refs_0_, bf16[32,32,128]{2,1,0:T(8,128)(2,1)S(1)} %all_to_all.15.refs_1_, f32[2,1,4,512]{3,2,1,0:T(4,128)S(1)} %get-tuple-element.17.refs_2_), custom_call_target="tpu_custom_call" | custom-call | flops 67108864 | bytes 1048576 | tf_op jit(solution)/shard_map/pallas_call | solution.py:506
  (4 shorter events, 0.0 us)
Async XLA Ops:
  0.6 0.9 %copy-start = (f32[2,128,128]{2,1,0:T(8,128)S(1)}, f32[2,128,128]{2,1,0:T(8,128)}, u32[]{:S(2)}) copy-start(f32[2,128,128]{2,1,0:T(8,128)} %constant.9.clone.refs_3_) | copy-start | bytes 393220
  1.5 0.9 %copy-start.1 = (f32[2,128,128]{2,1,0:T(8,128)S(1)}, f32[2,128,128]{2,1,0:T(8,128)}, u32[]{:S(2)}) copy-start(f32[2,128,128]{2,1,0:T(8,128)} %constant.8.clone.refs_2_) | copy-start | bytes 393220
  2.4 0.7 %copy-start.4 = (f32[1,4096]{1,0:T(1,128)S(1)}, f32[1,4096]{1,0:T(1,128)}, u32[]{:S(2)}) copy-start(f32[1,4096]{1,0:T(1,128)} %refs_1_.1) | copy-start | bytes 49156
  3.2 5.9 %copy-start.9 = (s32[1,4]{1,0:T(1,128)S(1)}, s32[1,4]{1,0:T(1,128)}, u32[]{:S(2)}) copy-start(s32[1,4]{1,0:T(1,128)} %positions.1) | copy-start | bytes 52
  8.4 8.3 %copy-start.2 = (f32[2,128,128]{2,1,0:T(8,128)S(1)}, f32[2,128,128]{2,1,0:T(8,128)}, u32[]{:S(2)}) copy-start(f32[2,128,128]{2,1,0:T(8,128)} %constant.11.clone.refs_3_) | copy-start | bytes 393220
  8.4 8.3 %copy-start.3 = (f32[2,128,128]{2,1,0:T(8,128)S(1)}, f32[2,128,128]{2,1,0:T(8,128)}, u32[]{:S(2)}) copy-start(f32[2,128,128]{2,1,0:T(8,128)} %constant.10.clone.refs_2_) | copy-start | bytes 393220
  8.4 19.2 %copy-start.7 = (s32[1,4,512]{2,1,0:T(4,128)S(1)}, s32[1,4,512]{2,1,0:T(4,128)}, u32[]{:S(2)}) copy-start(s32[1,4,512]{2,1,0:T(4,128)} %vis_u.1) | copy-start | bytes 24580
  8.4 19.2 %copy-start.8 = (s32[1,4,512]{2,1,0:T(4,128)S(1)}, s32[1,4,512]{2,1,0:T(4,128)}, u32[]{:S(2)}) copy-start(s32[1,4,512]{2,1,0:T(4,128)} %vis_v.1) | copy-start | bytes 24580
  8.4 19.2 %copy-start.10 = (f32[8]{0:T(128)S(1)}, f32[8]{0:T(128)}, u32[]{:S(2)}) copy-start(f32[8]{0:T(128)} %taps.1) | copy-start | bytes 100
  8.4 29.8 %copy-start.5 = (f32[2,1,4,512]{3,2,1,0:T(4,128)S(1)}, f32[2,1,4,512]{3,2,1,0:T(4,128)}, u32[]{:S(2)}) copy-start(f32[2,1,4,512]{3,2,1,0:T(4,128)} %observed.1) | copy-start | bytes 49156
  8.5 29.8 %copy-start.6 = (s32[1,4]{1,0:T(1,128)S(1)}, s32[1,4]{1,0:T(1,128)}, u32[]{:S(2)}) copy-start(s32[1,4]{1,0:T(1,128)} %counts.1) | copy-start | bytes 52
  8.5 8.2 %collective-permute-start = (bf16[512,128]{1,0:T(8,128)(2,1)S(1)}, bf16[512,128]{1,0:T(8,128)(2,1)S(1)}, u32[]{:S(2)}, u32[]{:S(2)}) collective-permute-start(bf16[512,128]{1,0:T(8,128)(2,1)S(1)} %get-tuple-element.13), channel_id=1, source_target_pairs={{0,1},{1,0},{2,3},{3,2},{4,5},{5,4},{6,7},{7,6},{8,9},{9,8},{10,11... | collective-permute-start | bytes 393224 | tf_op jit(solution)/shard_map/ppermute | solution.py:560
  9.7 14.1 %all-to-all-start = ((s32[32,1,128]{2,1,0:T(1,128)}), s32[32,1,128]{2,1,0:T(1,128)S(1)}, u32[]{:S(2)}, u32[]{:S(2)}) async-start(s32[32,1,128]{2,1,0:T(1,128)} %get-tuple-element.10), calls=%async_computation | async-start | bytes 32768 | tf_op jit(solution)/shard_map/all_to_all | solution.py:518
  25.1 13.2 %all-to-all-start.1 = ((bf16[32,32,128]{2,1,0:T(8,128)(2,1)}), bf16[32,32,128]{2,1,0:T(8,128)(2,1)S(1)}, u32[]{:S(2)}, u32[]{:S(2)}) async-start(bf16[32,32,128]{2,1,0:T(8,128)(2,1)} %shard_map.134), calls=%async_computation.1 | async-start | bytes 524288 | tf_op jit(solution)/shard_map/all_to_all | solution.py:518
